TPU v7x, 8 devices: a whole 2x2x1 slice. The times are simulated.
8 devices in a mesh: tp: 4 (over z, y, x), cp: 2 (over core).
Axes of the slice: x: 2, y: 2, z: 1, core: 2. Of those that a mesh axis runs over, the one named last changes fastest.
Arguments:
- hidden: bfloat16 [3, 1024, 5120], P(None, 'cp')
- grad_out: bfloat16 [3, 1024, 5120], P(None, 'cp')
- w_dq: bfloat16 [5120, 1536], replicated
- g_q: bfloat16 [1536], replicated
- w_dkv: bfloat16 [5120, 576], replicated
- g_kv: bfloat16 [512], replicated
- w_uq: bfloat16 [1536, 128, 192], P(None, 'tp')
- w_uk: bfloat16 [512, 128, 128], P(None, 'tp')
- w_uv: bfloat16 [512, 128, 128], P(None, 'tp')
- w_o: bfloat16 [128, 128, 5120], P('tp')
Outputs:
- output 1: bfloat16 [3, 1024, 5120], P(None, 'cp')
- output 2: bfloat16 [3, 1024, 5120], P(None, 'cp')
- output 3: float32 [5120, 1536], replicated
- output 4: float32 [1536], replicated
- output 5: float32 [5120, 576], replicated
- output 6: float32 [512], replicated
- output 7: float32 [1536, 128, 192], P(None, 'tp')
- output 8: float32 [512, 128, 128], P(None, 'tp')
- output 9: float32 [512, 128, 128], P(None, 'tp')
- output 10: float32 [128, 128, 5120], P('tp')
All inputs are finite; a program needn't handle non-finite values.
Results may differ from a plain program's by a relative error of at most 0.014927.
Values are sent between devices in bfloat16 or wider.
A program may use at most 1.25 GiB of HBM per device.

v0:
```python
import jax
import jax.numpy as jnp
from jax import lax
from jax.sharding import PartitionSpec as P

EPS = 1e-6
THETA = 10000.0
NEG_BIG = -1e30


def layout_positions(seq_local, cp_size, cp_rank):
    half_len = seq_local // 2
    local_idx = jnp.arange(seq_local, dtype=jnp.int32)
    block_id = jnp.where(local_idx < half_len, cp_rank, 2 * cp_size - 1 - cp_rank)
    return block_id * half_len + local_idx % half_len


def rope_tables(positions, rope_dim):
    inv_freq = 1.0 / (THETA ** (jnp.arange(rope_dim // 2, dtype=jnp.float32) * 2.0 / rope_dim))
    angles = positions.astype(jnp.float32)[:, None] * inv_freq[None, :]
    return jnp.cos(angles), jnp.sin(angles)


def apply_rope(values, cos_tab, sin_tab):
    half_dim = values.shape[-1] // 2
    lead_half = values[..., :half_dim]
    tail_half = values[..., half_dim:]
    return jnp.concatenate([lead_half * cos_tab - tail_half * sin_tab, tail_half * cos_tab + lead_half * sin_tab], axis=-1)


def unrope(grad_vals, cos_tab, sin_tab):
    half_dim = grad_vals.shape[-1] // 2
    lead_half = grad_vals[..., :half_dim]
    tail_half = grad_vals[..., half_dim:]
    return jnp.concatenate([lead_half * cos_tab + tail_half * sin_tab, tail_half * cos_tab - lead_half * sin_tab], axis=-1)


def norm_f32(raw_vals, gain_vec):
    inv_rms = lax.rsqrt(jnp.mean(raw_vals * raw_vals, axis=-1, keepdims=True) + EPS)
    return raw_vals * inv_rms * gain_vec


def solution(mesh):
    cp_size = mesh.shape['cp']
    next_pairs = [(src_idx, (src_idx + 1) % cp_size) for src_idx in range(cp_size)]

    def per_device(hidden, grad_out, w_dq, g_q, w_dkv, g_kv, w_uq, w_uk, w_uv, w_o):
        cp_rank = lax.axis_index('cp')
        n_batch = hidden.shape[0]
        seq_local = hidden.shape[1]
        value_a6 = w_dq.shape[1]
        value_a7 = g_kv.shape[0]
        nope_dim = w_uk.shape[2]
        qk_dim = w_uq.shape[2]
        heads_dev = w_uq.shape[1]
        v_dim = w_uv.shape[2]
        score_scale = qk_dim ** -0.5
        positions = layout_positions(seq_local, cp_size, cp_rank)
        cos_tab, sin_tab = rope_tables(positions, qk_dim - nope_dim)
        cos_head = cos_tab[:, None, :]
        sin_head = sin_tab[:, None, :]

        cq_raw = jnp.einsum('btd,dq->btq', hidden, w_dq, preferred_element_type=jnp.float32).astype(jnp.bfloat16)
        kv_raw = jnp.einsum('btd,dc->btc', hidden, w_dkv, preferred_element_type=jnp.float32).astype(jnp.bfloat16)
        cq_f32 = cq_raw.astype(jnp.float32)
        ckv_f32 = kv_raw[..., :value_a7].astype(jnp.float32)
        gq_f32 = g_q.astype(jnp.float32)
        gkv_f32 = g_kv.astype(jnp.float32)
        c_q = norm_f32(cq_f32, gq_f32).astype(jnp.bfloat16)
        c_kv = norm_f32(ckv_f32, gkv_f32).astype(jnp.bfloat16)
        k_pe = apply_rope(kv_raw[..., value_a7:].astype(jnp.float32), cos_tab, sin_tab).astype(jnp.bfloat16)
        q_all = jnp.einsum('btq,qhe->bthe', c_q, w_uq, preferred_element_type=jnp.float32).astype(jnp.bfloat16)
        q_nope = q_all[..., :nope_dim]
        q_pe = apply_rope(q_all[..., nope_dim:].astype(jnp.float32), cos_head, sin_head).astype(jnp.bfloat16)
        k_nope = jnp.einsum('btc,chn->bthn', c_kv, w_uk, preferred_element_type=jnp.float32).astype(jnp.bfloat16)
        v_heads = jnp.einsum('btc,chv->bthv', c_kv, w_uv, preferred_element_type=jnp.float32).astype(jnp.bfloat16)

        def block_scores(kn_blk, kp_blk, src_rank):
            key_pos = layout_positions(seq_local, cp_size, src_rank)
            scores = jnp.einsum('bqhn,bkhn->bhqk', q_nope, kn_blk, preferred_element_type=jnp.float32) + jnp.einsum('bqhr,bkr->bhqk', q_pe, kp_blk, preferred_element_type=jnp.float32)
            return jnp.where(key_pos[None, :] <= positions[:, None], scores * score_scale, NEG_BIG)

        def attend(soft_stats, kn_blk, kp_blk, v_blk, src_rank):
            row_max, row_sum, out_acc = soft_stats
            scores = block_scores(kn_blk, kp_blk, src_rank)
            new_max = jnp.maximum(row_max, jnp.max(scores, axis=-1))
            rescale = jnp.exp(row_max - new_max)
            prob_blk = jnp.exp(scores - new_max[..., None])
            row_sum = row_sum * rescale + jnp.sum(prob_blk, axis=-1)
            out_acc = out_acc * rescale[..., None] + jnp.einsum('bhqk,bkhv->bhqv', prob_blk.astype(jnp.bfloat16), v_blk, preferred_element_type=jnp.float32)
            return new_max, row_sum, out_acc

        soft_stats = (jnp.full((n_batch, heads_dev, seq_local), NEG_BIG, jnp.float32), jnp.zeros((n_batch, heads_dev, seq_local), jnp.float32), jnp.zeros((n_batch, heads_dev, seq_local, v_dim), jnp.float32))
        soft_stats = attend(soft_stats, k_nope, k_pe, v_heads, cp_rank)

        def fwd_step(step_idx, loop_state):
            kn_blk, kp_blk, v_blk, soft_stats = loop_state
            kn_blk, kp_blk, v_blk = lax.ppermute((kn_blk, kp_blk, v_blk), 'cp', next_pairs)
            soft_stats = attend(soft_stats, kn_blk, kp_blk, v_blk, (cp_rank - step_idx) % cp_size)
            return kn_blk, kp_blk, v_blk, soft_stats

        loop_state = lax.fori_loop(1, cp_size, fwd_step, (k_nope, k_pe, v_heads, soft_stats))
        row_max, row_sum, out_acc = loop_state[3]
        o_heads = (out_acc / row_sum[..., None]).astype(jnp.bfloat16)
        log_sum = row_max + jnp.log(row_sum)
        attn_out = lax.psum(jnp.einsum('bhtv,hvd->btd', o_heads, w_o, preferred_element_type=jnp.float32), 'tp').astype(jnp.bfloat16)

        grad_o = jnp.einsum('btd,hvd->bhtv', grad_out, w_o, preferred_element_type=jnp.float32).astype(jnp.bfloat16)
        grad_w_o = jnp.einsum('bhtv,btd->hvd', o_heads, grad_out, preferred_element_type=jnp.float32)
        row_dot = jnp.einsum('bhtv,bhtv->bht', grad_o, o_heads, preferred_element_type=jnp.float32)

        def grad_block(kn_blk, kp_blk, v_blk, src_rank):
            prob_blk = jnp.exp(block_scores(kn_blk, kp_blk, src_rank) - log_sum[..., None])
            dv_part = jnp.einsum('bhqk,bhqv->bkhv', prob_blk.astype(jnp.bfloat16), grad_o, preferred_element_type=jnp.float32)
            dp_blk = jnp.einsum('bhqv,bkhv->bhqk', grad_o, v_blk, preferred_element_type=jnp.float32)
            ds_blk = (prob_blk * (dp_blk - row_dot[..., None]) * score_scale).astype(jnp.bfloat16)
            dqn_part = jnp.einsum('bhqk,bkhn->bqhn', ds_blk, kn_blk, preferred_element_type=jnp.float32)
            dqp_part = jnp.einsum('bhqk,bkr->bqhr', ds_blk, kp_blk, preferred_element_type=jnp.float32)
            dkn_part = jnp.einsum('bhqk,bqhn->bkhn', ds_blk, q_nope, preferred_element_type=jnp.float32)
            dkp_part = jnp.einsum('bhqk,bqhr->bkr', ds_blk, q_pe, preferred_element_type=jnp.float32)
            return dqn_part, dqp_part, dkn_part, dkp_part, dv_part

        own_parts = grad_block(k_nope, k_pe, v_heads, cp_rank)
        init_state = (k_nope, k_pe, v_heads, own_parts[2].astype(jnp.bfloat16), own_parts[3].astype(jnp.bfloat16), own_parts[4].astype(jnp.bfloat16), own_parts[0], own_parts[1])

        def bwd_step(step_idx, loop_state):
            kn_blk, kp_blk, v_blk, dkn_blk, dkp_blk, dv_blk, dq_nope, dq_pe = loop_state
            kn_blk, kp_blk, v_blk, dkn_blk, dkp_blk, dv_blk = lax.ppermute((kn_blk, kp_blk, v_blk, dkn_blk, dkp_blk, dv_blk), 'cp', next_pairs)
            step_parts = grad_block(kn_blk, kp_blk, v_blk, (cp_rank - step_idx) % cp_size)
            return (kn_blk, kp_blk, v_blk,
                    (dkn_blk.astype(jnp.float32) + step_parts[2]).astype(jnp.bfloat16),
                    (dkp_blk.astype(jnp.float32) + step_parts[3]).astype(jnp.bfloat16),
                    (dv_blk.astype(jnp.float32) + step_parts[4]).astype(jnp.bfloat16),
                    dq_nope + step_parts[0], dq_pe + step_parts[1])

        loop_state = lax.fori_loop(1, cp_size, bwd_step, init_state)
        grad_k_nope, grad_k_pe, grad_v = lax.ppermute((loop_state[3], loop_state[4], loop_state[5]), 'cp', next_pairs)
        grad_q = jnp.concatenate([loop_state[6], unrope(loop_state[7], cos_head, sin_head)], axis=-1).astype(jnp.bfloat16)

        grad_w_uq = jnp.einsum('btq,bthe->qhe', c_q, grad_q, preferred_element_type=jnp.float32)
        grad_w_uk = jnp.einsum('btc,bthn->chn', c_kv, grad_k_nope, preferred_element_type=jnp.float32)
        grad_w_uv = jnp.einsum('btc,bthv->chv', c_kv, grad_v, preferred_element_type=jnp.float32)
        latent_part = jnp.concatenate([
            jnp.einsum('bthe,qhe->btq', grad_q, w_uq, preferred_element_type=jnp.float32),
            jnp.einsum('bthn,chn->btc', grad_k_nope, w_uk, preferred_element_type=jnp.float32) + jnp.einsum('bthv,chv->btc', grad_v, w_uv, preferred_element_type=jnp.float32),
            grad_k_pe.astype(jnp.float32)], axis=-1)
        latent_grad = lax.psum(latent_part, 'tp')

        norm_q_pull = jax.vjp(norm_f32, cq_f32, gq_f32)[1]
        grad_cq_raw, grad_g_q = norm_q_pull(latent_grad[..., :value_a6])
        norm_kv_pull = jax.vjp(norm_f32, ckv_f32, gkv_f32)[1]
        grad_ckv_raw, grad_g_kv = norm_kv_pull(latent_grad[..., value_a6:value_a6 + value_a7])
        grad_kv_raw = jnp.concatenate([grad_ckv_raw, unrope(latent_grad[..., value_a6 + value_a7:], cos_tab, sin_tab)], axis=-1).astype(jnp.bfloat16)
        grad_cq_raw = grad_cq_raw.astype(jnp.bfloat16)
        grad_w_dq = jnp.einsum('btd,btq->dq', hidden, grad_cq_raw, preferred_element_type=jnp.float32)
        grad_w_dkv = jnp.einsum('btd,btc->dc', hidden, grad_kv_raw, preferred_element_type=jnp.float32)
        grad_hidden = (jnp.einsum('btq,dq->btd', grad_cq_raw, w_dq, preferred_element_type=jnp.float32) + jnp.einsum('btc,dc->btd', grad_kv_raw, w_dkv, preferred_element_type=jnp.float32)).astype(jnp.bfloat16)
        weight_grads = lax.psum((grad_w_dq, grad_g_q, grad_w_dkv, grad_g_kv, grad_w_uq, grad_w_uk, grad_w_uv, grad_w_o), 'cp')
        return (attn_out, grad_hidden) + tuple(weight_grads)

    seq_spec = P(None, 'cp', None)
    full_spec = P()
    head_spec = P(None, 'tp', None)
    out_head_spec = P('tp', None, None)
    all_specs = (seq_spec, seq_spec, full_spec, full_spec, full_spec, full_spec, head_spec, head_spec, head_spec, out_head_spec)
    return jax.shard_map(per_device, mesh=mesh, in_specs=all_specs, out_specs=all_specs, check_vma=False)
```

profile of v0, /device:TPU:0, one launch (start us, length us, event | category | flops | bytes accessed | tf_op | source)
XLA Modules:
  0.0 2817.5 jit_solution(14599072396614646737)
XLA Ops:
  50.2 32.5 %fusion.52 = (f32[3,512]{1,0:T(4,128)S(1)}, bf16[3,512,1536]{2,1,0:T(8,128)(2,1)S(1)}) fusion(bf16[3,512,5120]{2,1,0:T(8,128)(2,1)} %param.10, bf16[5120,1536]{1,0:T(8,128)(2,1)} %param.12), kind=kOutput, calls=%fused_computation.70 | convolution fusion | flops 24168626176 | bytes 36182016 | tf_op jit(solution)/shard_map/btd,dq->btq/dot_general | solution.py:63
  84.9 36.3 %fusion.44 = bf16[3,512,32,192]{1,3,2,0:T(8,128)(2,1)} fusion(bf16[1536,32,192]{0,2,1:T(8,128)(2,1)} %param.16, bf16[3,512,1536]{2,1,0:T(8,128)(2,1)S(1)} %get-tuple-element.147, f32[1536]{0:T(1024)S(1)} %convert_element_type.133, f32[3,512]{1,0:T(4,128)S(1)} %fusion.118), kind=kOutput, calls=%fused_computation.66 | convolution fusion | flops 29009903616 | bytes 42479616 | tf_op jit(solution)/shard_map/btq,qhe->bthe/dot_general | solution.py:72
  131.2 74.1 %convert_bitcast_fusion.2 = bf16[3,32,512,128]{2,3,0,1:T(8,128)(2,1)} fusion(bf16[3,512,5120]{2,1,0:T(8,128)(2,1)} %param.11, bf16[32,128,5120]{2,1,0:T(8,128)(2,1)} %param.19), kind=kOutput, calls=%fused_computation.63 | convolution fusion | flops 64430800896 | bytes 70254592 | tf_op jit(solution)/shard_map/btd,hvd->bhtv/dot_general | solution.py:108
  205.3 36.4 %fusion.116 = f32[3,512,512,32]{2,1,3,0:T(8,128)} fusion(bf16[3,512,64]{2,1,0:T(8,128)(2,1)} %pad_maximum_fusion.10, bf16[3,512,32,32]{1,3,2,0:T(8,128)(2,1)} %get-tuple-element.136, bf16[3,512,32,32]{1,3,2,0:T(8,128)(2,1)S(1)} %copy-done), kind=kOutput, calls=%fused_computation.142 | convolution fusion | flops 3233808384 | bytes 107151360 | tf_op jit(solution)/shard_map/bqhr,bkr->bhqk/dot_general | solution.py:80
  241.7 73.5 %fusion.134 = (f32[3,32,512]{2,1,0:T(8,128)}, f32[3,32,512,512]{2,3,1,0:T(8,128)}) fusion(f32[3,512,512,32]{2,1,3,0:T(8,128)} %fusion.116, bf16[3,512,32,128]{3,1,2,0:T(8,128)(2,1)} %convolution_convert_fusion.1, bf16[3,512,32,192]{1,3,2,0:T(8,128)(2,1)} %fusion.44, pred[512,512]{0,1:T(8,128)(4,1)S(1)} %copy-done.5), kind=kOutput, calls=%fused_computation.173 | convolution fusion | flops 6543065088 | bytes 226951168 | tf_op jit(solution)/shard_map/bqhn,bkhn->bhqk/dot_general | solution.py:80
  332.7 36.4 %fusion.112 = f32[3,512,512,32]{2,1,3,0:T(8,128)} fusion(bf16[3,512,64]{2,1,0:T(8,128)(2,1)} %collective-permute-done.1, bf16[3,512,32,32]{1,3,2,0:T(8,128)(2,1)} %get-tuple-element.136, bf16[3,512,32,32]{1,3,2,0:T(8,128)(2,1)S(1)} %copy-done), kind=kOutput, calls=%fused_computation.138 | convolution fusion | flops 3233808384 | bytes 107151360 | tf_op jit(solution)/shard_map/while/body/eval_jaxpr/bqhr,bkr->bhqk/dot_general | solution.py:80
  369.0 72.6 %fusion.135 = (f32[3,32,512]{2,1,0:T(8,128)S(1)}, f32[3,32,512,512]{2,3,1,0:T(8,128)}) fusion(f32[3,512,512,32]{2,1,3,0:T(8,128)} %fusion.112, bf16[3,512,32,128]{3,1,2,0:T(8,128)(2,1)} %collective-permute-done, bf16[3,512,32,192]{1,3,2,0:T(8,128)(2,1)} %fusion.44, pred[512,512]{0,1:T(8,128)(4,1)S(1)} %copy-done.4), kind=kOutput, calls=%fused_computation.174 | convolution fusion | flops 6543065088 | bytes 226951168 | tf_op jit(solution)/shard_map/while/body/eval_jaxpr/bqhn,bkhn->bhqk/dot_general | solution.py:80
  442.4 30.9 %fusion.4 = f32[3,32,512]{2,1,0:T(8,128)S(1)} fusion(f32[3,32,512,512]{2,3,1,0:T(8,128)} %get-tuple-element.149, f32[3,32,512]{2,1,0:T(8,128)S(1)} %get-tuple-element.141), kind=kLoop, calls=%fused_computation.12 | loop fusion | flops 50282496 | bytes 101056512 | tf_op jit(solution)/shard_map/reduce_sum | solution.py:89
  473.4 30.9 %fusion.6 = f32[3,32,512]{2,1,0:T(8,128)S(1)} fusion(f32[3,32,512,512]{2,3,1,0:T(8,128)} %get-tuple-element.151, f32[3,32,512]{2,1,0:T(8,128)S(1)} %get-tuple-element.140), kind=kLoop, calls=%fused_computation.14 | loop fusion | flops 50282496 | bytes 101056512 | tf_op jit(solution)/shard_map/while/body/eval_jaxpr/reduce_sum | solution.py:89
  504.4 41.2 %convert_bitcast_fusion = bf16[3,512,32,128]{1,3,2,0:T(8,128)(2,1)} fusion(f32[3,32,512,512]{2,3,1,0:T(8,128)} %get-tuple-element.149, f32[3,32,512]{2,1,0:T(8,128)S(1)} %get-tuple-element.128, bf16[3,32,512,128]{2,3,0,1:T(8,128)(2,1)} %convert_bitcast_fusion.2), kind=kOutput, calls=%fused_computation.60 | convolution fusion | flops 6499074048 | bytes 126025728 | tf_op jit(solution)/shard_map/bhqk,bhqv->bkhv/dot_general | solution.py:114
  545.6 45.7 %fusion.16 = f32[3,32,512,128]{3,2,1,0:T(8,128)} fusion(bf16[3,512,32,128]{3,1,2,0:T(8,128)(2,1)} %convolution_convert_fusion, f32[3,32,512,512]{2,3,1,0:T(8,128)} %get-tuple-element.149, f32[3,32,512]{2,1,0:T(8,128)S(1)} %get-tuple-element.141), kind=kOutput, calls=%fused_computation.21 | convolution fusion | flops 6492782592 | bytes 138608640 | tf_op jit(solution)/shard_map/bhqk,bkhv->bhqv/dot_general | solution.py:90
  591.4 62.0 %multiply_reduce_fusion = (f32[3,32,512]{2,1,0:T(8,128)S(1)}, bf16[3,32,512,128]{3,2,1,0:T(8,128)(2,1)}) fusion(f32[3,32,512,128]{3,2,1,0:T(8,128)} %copy.137, f32[3,32,512]{2,1,0:T(8,128)S(1)} %get-tuple-element.129, bf16[3,512,32,128]{3,1,2,0:T(8,128)(2,1)} %collective-permute-done.2, f32[3,32,512,512]{2,3,1,0:T(8,128)} %get-tuple-element.151, ...), kind=kOutput, calls=%fused_computation.36 | convolution fusion | flops 6543065088 | bytes 177143808 | tf_op jit(solution)/shard_map/while/body/eval_jaxpr/bhqk,bkhv->bhqv/dot_general | solution.py:90
  653.3 56.6 %multiply_convert_fusion.1 = bf16[3,32,512,512]{2,3,1,0:T(8,128)(2,1)} fusion(f32[3,32,512,512]{2,3,1,0:T(8,128)} %get-tuple-element.149, f32[3,32,512]{2,1,0:T(8,128)S(1)} %get-tuple-element.152, f32[3,32,512]{2,1,0:T(8,128)S(1)} %get-tuple-element.128, bf16[3,512,32,128]{3,1,2,0:T(8,128)(2,1)} %convolution_convert_fusion, ...), kind=kOutput, calls=%fused_computation.8 | convolution fusion | flops 6568280064 | bytes 176553984 | tf_op jit(solution)/shard_map/bhqv,bkhv->bhqk/dot_general | solution.py:115
  732.2 29.7 %convert_bitcast_fusion.1 = bf16[3,512,32,128]{1,3,2,0:T(8,128)(2,1)} fusion(bf16[3,32,512,512]{2,3,1,0:T(8,128)(2,1)} %multiply_convert_fusion.1, bf16[3,512,32,192]{1,3,2,0:T(8,128)(2,1)} %fusion.44), kind=kOutput, calls=%fused_computation.61 | convolution fusion | flops 6448742400 | bytes 75497472 | tf_op jit(solution)/shard_map/bhqk,bqhn->bkhn/dot_general | solution.py:119
  762.5 56.5 %multiply_convert_fusion = bf16[3,32,512,512]{2,3,1,0:T(8,128)(2,1)} fusion(f32[3,32,512,512]{2,3,1,0:T(8,128)} %get-tuple-element.151, f32[3,32,512]{2,1,0:T(8,128)S(1)} %get-tuple-element.152, f32[3,32,512]{2,1,0:T(8,128)S(1)} %get-tuple-element.128, bf16[3,512,32,128]{3,1,2,0:T(8,128)(2,1)} %collective-permute-done.2, ...), kind=kOutput, calls=%fused_computation.6 | convolution fusion | flops 6568280064 | bytes 176553984 | tf_op jit(solution)/shard_map/while/body/eval_jaxpr/bhqv,bkhv->bhqk/dot_general | solution.py:115
  819.0 30.5 %fusion.136 = f32[3,32,128,512]{3,2,1,0:T(8,128)} fusion(bf16[3,512,32,128]{3,1,2,0:T(8,128)(2,1)} %convolution_convert_fusion.1, bf16[3,32,512,512]{2,3,1,0:T(8,128)(2,1)} %multiply_convert_fusion.1), kind=kOutput, calls=%fused_computation.175 | convolution fusion | flops 6442450944 | bytes 88080384 | tf_op jit(solution)/shard_map/bhqk,bkhn->bqhn/dot_general | solution.py:117
  849.5 33.0 %fusion.41 = bf16[3,512,32,128]{1,3,2,0:T(8,128)(2,1)} fusion(f32[3,32,128,512]{3,2,1,0:T(8,128)} %fusion.136, bf16[3,512,32,128]{3,1,2,0:T(8,128)(2,1)} %collective-permute-done, bf16[3,32,512,512]{2,3,1,0:T(8,128)(2,1)} %multiply_convert_fusion), kind=kOutput, calls=%fused_computation.59 | convolution fusion | flops 6455033856 | bytes 100663296 | tf_op jit(solution)/shard_map/while/body/eval_jaxpr/bhqk,bkhn->bqhn/dot_general | solution.py:117
  882.5 45.0 %fusion.26 = bf16[3,512,32,128]{1,3,2,0:T(8,128)(2,1)} fusion(bf16[3,512,32,128]{1,3,2,0:T(8,128)(2,1)} %collective-permute-done.5, f32[3,32,512,512]{2,3,1,0:T(8,128)} %get-tuple-element.151, f32[3,32,512]{2,1,0:T(8,128)S(1)} %get-tuple-element.128, bf16[3,32,512,128]{2,3,0,1:T(8,128)(2,1)} %convert_bitcast_fusion.2), kind=kOutput, calls=%fused_computation.33 | convolution fusion | flops 6511656960 | bytes 138608640 | tf_op jit(solution)/shard_map/while/body/eval_jaxpr/bhqk,bhqv->bkhv/dot_general | solution.py:114
  928.0 31.6 %fusion.27 = bf16[3,512,32,128]{1,3,2,0:T(8,128)(2,1)} fusion(bf16[3,512,32,128]{1,3,2,0:T(8,128)(2,1)} %collective-permute-done.3, bf16[3,32,512,512]{2,3,1,0:T(8,128)(2,1)} %multiply_convert_fusion, bf16[3,512,32,192]{1,3,2,0:T(8,128)(2,1)} %fusion.44), kind=kOutput, calls=%fused_computation.35 | convolution fusion | flops 6461325312 | bytes 88080384 | tf_op jit(solution)/shard_map/while/body/eval_jaxpr/bhqk,bqhn->bkhn/dot_general | solution.py:119
  982.6 27.6 add_bitcast_fusion
  1039.8 39.3 %fusion.78 = f32[3,512,1536]{2,1,0:T(8,128)} fusion(bf16[1536,32,192]{0,2,1:T(8,128)(2,1)} %param.16, bf16[3,512,32,32]{1,3,2,0:T(8,128)(2,1)} %get-tuple-element.134, bf16[3,512,32,32]{1,3,2,0:T(8,128)(2,1)} %get-tuple-element.133, bf16[3,512,32,128]{1,3,2,0:T(8,128)(2,1)} %fusion.41), kind=kOutput, calls=%fused_computation.98 | convolution fusion | flops 29047652352 | bytes 47185920 | tf_op jit(solution)/shard_map/bthe,qhe->btq/dot_general | solution.py:144
  1112.6 39.1 %convolution_bitcast_fusion.2 = f32[1536,32,192]{0,2,1:T(8,128)} fusion(bf16[3,512,32,32]{1,3,2,0:T(8,128)(2,1)} %get-tuple-element.134, bf16[3,512,32,32]{1,3,2,0:T(8,128)(2,1)} %get-tuple-element.133, bf16[3,512,32,128]{1,3,2,0:T(8,128)(2,1)} %fusion.41, bf16[3,512,1536]{2,1,0:T(8,128)(2,1)} %copy-done.6, f32[1536]{0:T(1024)S(1)} %copy-done.28, ...), kind=kOutput, calls=%fused_computation.45 | convolution fusion | flops 29057089536 | bytes 61353984 | tf_op jit(solution)/shard_map/btq,bthe->qhe/dot_general | solution.py:140
  1176.9 177.7 %all-reduce.7.cloned.1.call-done = f32[3,512,2112]{2,1,0:T(8,128)} async-done(((f32[3,512,2112]{2,1,0:T(8,128)}), f32[3,512,2112]{2,1,0:T(8,128)}) %all-reduce.7.cloned.1.call-update) | async-done | bytes 12976144 | tf_op jit(solution)/shard_map/psum | solution.py:147
  1369.5 33.0 %convolution_bitcast_fusion.1 = f32[5120,1536]{0,1:T(8,128)} fusion(bf16[3,512,1536]{2,1,0:T(8,128)(2,1)S(1)} %fusion.51, bf16[3,512,5120]{2,1,0:T(8,128)(2,1)} %param.10), kind=kOutput, calls=%fused_computation.39 | convolution fusion | flops 24159191040 | bytes 51904512 | tf_op jit(solution)/shard_map/btd,btq->dq/dot_general | solution.py:155
  1421.3 75.6 %convolution_bitcast_fusion = f32[32,128,5120]{2,1,0:T(8,128)} fusion(bf16[3,32,512,128]{3,2,1,0:T(8,128)(2,1)} %get-tuple-element.153, bf16[3,512,5120]{2,1,0:T(8,128)(2,1)} %param.11), kind=kOutput, calls=%fused_computation.26 | convolution fusion | flops 64424509440 | bytes 112197632 | tf_op jit(solution)/shard_map/bhtv,btd->hvd/dot_general | solution.py:109
  1496.9 74.2 %fusion.38 = f32[3,512,5120]{2,1,0:T(8,128)} fusion(bf16[3,32,512,128]{3,2,1,0:T(8,128)(2,1)} %get-tuple-element.153, bf16[32,128,5120]{2,1,0:T(8,128)(2,1)} %param.19), kind=kOutput, calls=%fused_computation.57 | convolution fusion | flops 64424509440 | bytes 85983232 | tf_op jit(solution)/shard_map/bhtv,hvd->btd/dot_general | solution.py:106
  1571.1 1035.3 %all-reduce.12 = bf16[3,512,5120]{2,1,0:T(8,128)(2,1)} all-reduce(f32[3,512,5120]{2,1,0:T(8,128)} %fusion.38), channel_id=1, replica_groups=mesh['tp'=4,'cp'=2] {'tp'}, use_global_device_ids=true, to_apply=%region_6.7 | all-reduce | flops 7864320 | bytes 47185920 | tf_op jit(solution)/shard_map/psum | solution.py:106
  2610.7 31.7 %fusion.34 = f32[3,512,5120]{2,1,0:T(8,128)} fusion(bf16[3,512,1536]{2,1,0:T(8,128)(2,1)} %copy-done.10, bf16[5120,1536]{1,0:T(8,128)(2,1)} %param.12), kind=kOutput, calls=%fused_computation.52 | convolution fusion | flops 24159191040 | bytes 51904512 | tf_op jit(solution)/shard_map/btq,dq->btd/dot_general | solution.py:157
  2642.4 23.9 add_convert_fusion
  2666.3 30.9 %copy.118 = f32[5120,1536]{1,0:T(8,128)} copy(f32[5120,1536]{0,1:T(8,128)} %get-tuple-element.123) | data formatting | bytes 62914560
  2727.6 28.8 %copy.229 = f32[1536,32,192]{0,2,1:T(8,128)} copy(f32[1536,32,192]{0,2,1:T(8,128)} %get-tuple-element.162) | data formatting | bytes 75497472
  2756.4 54.2 %copy.230 = f32[32,128,5120]{2,1,0:T(8,128)} copy(f32[32,128,5120]{2,1,0:T(8,128)} %all-reduce.9.cloned.1.call-done) | data formatting | bytes 167772160
  (179 shorter events, 276.1 us)
Async XLA Ops:
  7.2 1347.4 %all-reduce.7.cloned.1.call-start = ((), (), s32[]{:S(2)}) async-start(), calls=%async_computation | async-start | bytes 26738688 | tf_op jit(solution)/shard_map/psum | solution.py:147
  7.6 118.3 %copy-start.18 = (f32[512,32]{0,1:T(8,128)}, f32[512,32]{0,1:T(8,128)S(1)}, u32[]{:S(2)}) copy-start(f32[512,32]{0,1:T(8,128)S(1)} %get-tuple-element.142) | copy-start | bytes 196612
  7.6 118.3 %copy-start.20 = (f32[512,32]{0,1:T(8,128)}, f32[512,32]{0,1:T(8,128)S(1)}, u32[]{:S(2)}) copy-start(f32[512,32]{0,1:T(8,128)S(1)} %get-tuple-element.143) | copy-start | bytes 196612
  26.5 306.1 %collective-permute-start.1 = (bf16[3,512,64]{2,1,0:T(8,128)(2,1)}, bf16[3,512,64]{2,1,0:T(8,128)(2,1)}, u32[]{:S(2)}, u32[]{:S(2)}) collective-permute-start(bf16[3,512,64]{2,1,0:T(8,128)(2,1)} %pad_maximum_fusion.10), channel_id=1, source_target_pairs={{0,1},{1,0},{2,3},{3,2},{4,5},{5,4},{6,7},{7,6}} | collective-permute-start | bytes 589832 | tf_op jit(solution)/shard_map/while/body/eval_jaxpr/ppermute | solution.py:98
  38.8 330.3 %collective-permute-start = (bf16[3,512,32,128]{3,1,2,0:T(8,128)(2,1)}, bf16[3,512,32,128]{3,1,2,0:T(8,128)(2,1)}, u32[]{:S(2)}, u32[]{:S(2)}) collective-permute-start(bf16[3,512,32,128]{3,1,2,0:T(8,128)(2,1)} %convolution_convert_fusion.1), channel_id=1, source_target_pairs={{0,1},{1,0},{2,3},{3,2},{4,5},{5,4},{6,7},{7,6}} | collective-permute-start | bytes 37748744 | tf_op jit(solution)/shard_map/while/body/eval_jaxpr/ppermute | solution.py:98
  49.7 541.6 %collective-permute-start.2 = (bf16[3,512,32,128]{3,1,2,0:T(8,128)(2,1)}, bf16[3,512,32,128]{3,1,2,0:T(8,128)(2,1)}, u32[]{:S(2)}, u32[]{:S(2)}) collective-permute-start(bf16[3,512,32,128]{3,1,2,0:T(8,128)(2,1)} %convolution_convert_fusion), channel_id=1, source_target_pairs={{0,1},{1,0},{2,3},{3,2},{4,5},{5,4},{6,7},{7,6}} | collective-permute-start | bytes 37748744 | tf_op jit(solution)/shard_map/while/body/eval_jaxpr/ppermute | solution.py:98
  50.2 33.1 %copy-start.27 = (f32[1536]{0:T(1024)}, f32[1536]{0:T(1024)S(1)}, u32[]{:S(2)}) copy-start(f32[1536]{0:T(1024)S(1)} %convert_element_type.133) | copy-start | bytes 18436
  131.2 74.1 %copy-start = (bf16[3,512,32,32]{1,3,2,0:T(8,128)(2,1)S(1)}, bf16[3,512,32,32]{1,3,2,0:T(8,128)(2,1)}, u32[]{:S(2)}) copy-start(bf16[3,512,32,32]{1,3,2,0:T(8,128)(2,1)} %get-tuple-element.135) | copy-start | bytes 9437188
  205.3 36.4 %copy-start.5 = (pred[512,512]{0,1:T(8,128)(4,1)S(1)}, pred[512,512]{0,1:T(8,128)(4,1)}, u32[]{:S(2)}) copy-start(pred[512,512]{0,1:T(8,128)(4,1)} %get-tuple-element.145) | copy-start | bytes 786436
  332.7 36.4 %copy-start.4 = (pred[512,512]{0,1:T(8,128)(4,1)S(1)}, pred[512,512]{0,1:T(8,128)(4,1)}, u32[]{:S(2)}) copy-start(pred[512,512]{0,1:T(8,128)(4,1)} %get-tuple-element.144) | copy-start | bytes 786436
  369.0 72.7 %copy-start.15 = (f32[3,32,512]{2,1,0:T(8,128)S(1)}, f32[3,32,512]{2,1,0:T(8,128)}, u32[]{:S(2)}) copy-start(f32[3,32,512]{2,1,0:T(8,128)} %get-tuple-element.148) | copy-start | bytes 589828
  545.6 45.7 %copy-start.26 = (f32[3,32,512]{2,1,0:T(8,128)S(1)}, f32[3,32,512]{2,1,0:T(8,128)}, u32[]{:S(2)}) copy-start(f32[3,32,512]{2,1,0:T(8,128)} %get-tuple-element.139) | copy-start | bytes 589828
  653.3 56.6 %copy-start.1 = (bf16[3,512,32,32]{1,3,2,0:T(8,128)(2,1)S(1)}, bf16[3,512,32,32]{1,3,2,0:T(8,128)(2,1)}, u32[]{:S(2)}) copy-start(bf16[3,512,32,32]{1,3,2,0:T(8,128)(2,1)} %get-tuple-element.135) | copy-start | bytes 9437188
  762.0 120.5 %collective-permute-start.5 = (bf16[3,512,32,128]{1,3,2,0:T(8,128)(2,1)}, bf16[3,512,32,128]{1,3,2,0:T(8,128)(2,1)}, u32[]{:S(2)}, u32[]{:S(2)}) collective-permute-start(bf16[3,512,32,128]{1,3,2,0:T(8,128)(2,1)} %convert_bitcast_fusion), channel_id=1, source_target_pairs={{0,1},{1,0},{2,3},{3,2},{4,5},{5,4},{6,7},{7,6}} | collective-permute-start | bytes 37748744 | tf_op jit(solution)/shard_map/while/body/eval_jaxpr/ppermute | solution.py:128
  762.0 255.8 %collective-permute-start.7 = (bf16[3,512,64]{1,2,0:T(8,128)(2,1)}, bf16[3,512,64]{1,2,0:T(8,128)(2,1)}, u32[]{:S(2)}, u32[]{:S(2)}) collective-permute-start(bf16[3,512,64]{1,2,0:T(8,128)(2,1)} %fusion.110), channel_id=1, source_target_pairs={{0,1},{1,0},{2,3},{3,2},{4,5},{5,4},{6,7},{7,6}} | collective-permute-start | bytes 589832 | tf_op jit(solution)/shard_map/while/body/eval_jaxpr/ppermute | solution.py:128
  762.5 165.5 %collective-permute-start.3 = (bf16[3,512,32,128]{1,3,2,0:T(8,128)(2,1)}, bf16[3,512,32,128]{1,3,2,0:T(8,128)(2,1)}, u32[]{:S(2)}, u32[]{:S(2)}) collective-permute-start(bf16[3,512,32,128]{1,3,2,0:T(8,128)(2,1)} %convert_bitcast_fusion.1), channel_id=1, source_target_pairs={{0,1},{1,0},{2,3},{3,2},{4,5},{5,4},{6,7},{7,6}} | collective-permute-start | bytes 37748744 | tf_op jit(solution)/shard_map/while/body/eval_jaxpr/ppermute | solution.py:128
  927.4 166.1 %collective-permute-start.6 = (bf16[3,512,32,128]{1,3,2,0:T(8,128)(2,1)}, bf16[3,512,32,128]{1,3,2,0:T(8,128)(2,1)}, u32[]{:S(2)}, u32[]{:S(2)}) collective-permute-start(bf16[3,512,32,128]{1,3,2,0:T(8,128)(2,1)} %fusion.26), channel_id=1, source_target_pairs={{0,1},{1,0},{2,3},{3,2},{4,5},{5,4},{6,7},{7,6}} | collective-permute-start | bytes 37748744 | tf_op jit(solution)/shard_map/ppermute | solution.py:137
  959.6 119.7 %collective-permute-start.4 = (bf16[3,512,32,128]{1,3,2,0:T(8,128)(2,1)}, bf16[3,512,32,128]{1,3,2,0:T(8,128)(2,1)}, u32[]{:S(2)}, u32[]{:S(2)}) collective-permute-start(bf16[3,512,32,128]{1,3,2,0:T(8,128)(2,1)} %fusion.27), channel_id=1, source_target_pairs={{0,1},{1,0},{2,3},{3,2},{4,5},{5,4},{6,7},{7,6}} | collective-permute-start | bytes 37748744 | tf_op jit(solution)/shard_map/ppermute | solution.py:137
  1039.3 39.8 %collective-permute-start.8 = (bf16[3,512,64]{1,2,0:T(8,128)(2,1)S(1)}, bf16[3,512,64]{1,2,0:T(8,128)(2,1)S(1)}, u32[]{:S(2)}, u32[]{:S(2)}) collective-permute-start(bf16[3,512,64]{1,2,0:T(8,128)(2,1)S(1)} %add_convert_fusion.6), channel_id=1, source_target_pairs={{0,1},{1,0},{2,3},{3,2},{4,5},{5,4},{6,7},{7,6}} | collective-permute-start | bytes 589832 | tf_op jit(solution)/shard_map/ppermute | solution.py:137
  1111.9 1554.4 %all-reduce.11.cloned.1.call-start = ((), (), s32[]{:S(2)}) async-start(), calls=%async_computation.2 | async-start | bytes 195559424 | tf_op jit(solution)/shard_map/psum | solution.py:158
  1112.6 39.1 %copy-start.9 = (bf16[3,512,576]{2,1,0:T(8,128)(2,1)S(1)}, bf16[3,512,576]{2,1,0:T(8,128)(2,1)}, u32[]{:S(2)}) copy-start(bf16[3,512,576]{2,1,0:T(8,128)(2,1)} %copy-done.8) | copy-start | bytes 5308420
  1112.6 39.1 %copy-start.34 = (f32[3,512]{1,0:T(4,128)S(1)}, f32[3,512]{1,0:T(4,128)}, u32[]{:S(2)}) copy-start(f32[3,512]{1,0:T(4,128)} %copy-done.33) | copy-start | bytes 18436
  1112.6 39.1 %copy-start.41 = (f32[512]{0:T(512)S(1)}, f32[512]{0:T(512)}, u32[]{:S(2)}) copy-start(f32[512]{0:T(512)} %copy-done.40) | copy-start | bytes 6148
  1164.2 194.1 %copy-start.36 = (f32[3,512]{1,0:T(4,128)S(1)}, f32[3,512]{1,0:T(4,128)}, u32[]{:S(2)}) copy-start(f32[3,512]{1,0:T(4,128)} %copy-done.35) | copy-start | bytes 18436
  1164.2 194.1 %copy-start.29 = (f32[1536]{0:T(1024)S(1)}, f32[1536]{0:T(1024)}, u32[]{:S(2)}) copy-start(f32[1536]{0:T(1024)} %copy-done.27) | copy-start | bytes 18436
  1164.2 194.1 %copy-start.32 = (f32[3,512]{1,0:T(4,128)S(1)}, f32[3,512]{1,0:T(4,128)}, u32[]{:S(2)}) copy-start(f32[3,512]{1,0:T(4,128)} %copy-done.30) | copy-start | bytes 18436
  1176.9 190.4 %copy-start.39 = (f32[3,512]{1,0:T(4,128)S(1)}, f32[3,512]{1,0:T(4,128)}, u32[]{:S(2)}) copy-start(f32[3,512]{1,0:T(4,128)} %copy-done.38) | copy-start | bytes 18436
  1369.5 33.1 %copy-start.10 = (bf16[3,512,1536]{2,1,0:T(8,128)(2,1)}, bf16[3,512,1536]{2,1,0:T(8,128)(2,1)S(1)}, u32[]{:S(2)}) copy-start(bf16[3,512,1536]{2,1,0:T(8,128)(2,1)S(1)} %fusion.51) | copy-start | bytes 14155780
  1369.5 33.1 %copy-start.12 = (f32[512,32]{1,0:T(8,128)S(1)}, f32[512,32]{1,0:T(8,128)}, u32[]{:S(2)}) copy-start(f32[512,32]{1,0:T(8,128)} %copy-done.11) | copy-start | bytes 196612
  1421.3 1296.0 %all-reduce.9.cloned.1.call-start = ((), (), s32[]{:S(2)}) async-start(), calls=%async_computation.1 | async-start | bytes 167772160 | tf_op jit(solution)/shard_map/psum | solution.py:158
  1571.1 1035.4 %copy-start.37 = (f32[1536]{0:T(1024)S(1)}, f32[1536]{0:T(1024)}, u32[]{:S(2)}) copy-start(f32[1536]{0:T(1024)} %get-tuple-element.117) | copy-start | bytes 18436
  1571.1 1035.4 %copy-start.42 = (f32[512]{0:T(512)S(1)}, f32[512]{0:T(512)}, u32[]{:S(2)}) copy-start(f32[512]{0:T(512)} %get-tuple-element.119) | copy-start | bytes 6148
  (33 other events, 474.4 us)
Sparse Core Ops, SparseCore 0:
  1112.0 242.4 all-reduce.6
  1421.4 229.8 all-reduce.10
  1654.3 197.8 all-reduce.8
where the time goes:
time: 2830 us; the launch traced here: 2820 us
  matrix products  1310 us (46%)
  blocking collectives  1040 us (37%)
  waiting for transfers between devices  178 us (6%)
  local copies, waits for them, and re-layouts  166 us (6%)
  other arithmetic  104 us (4%)
    psum x1, blocking collectives, per_device(): lax.psum(jnp.einsum('bhtv,hvd->btd', o_heads, w_o, preferred_element_type...  1040 us
    psum x1, waiting for transfers between devices, per_device(): latent_grad = lax.psum(latent_part, 'tp')  178 us
    unnamed x113, local copies, waits for them, and re-layouts  166 us
    dot_general x2, matrix products, block_scores(): jnp.einsum('bqhn,bkhn->bhqk', q_nope, kn_blk, preferred_element_type=jnp....  146 us
    dot_general x2, matrix products, grad_block(): jnp.einsum('bhqv,bkhv->bhqk', grad_o, v_blk, preferred_element_type=jnp.f...  113 us
    dot_general x2, matrix products, attend(): jnp.einsum('bhqk,bkhv->bhqv', prob_blk.astype(jnp.bfloat16), v_blk, prefe...  108 us
    dot_general x2, matrix products, grad_block(): jnp.einsum('bhqk,bhqv->bkhv', prob_blk.astype(jnp.bfloat16), grad_o, pref...  86.1 us
    dot_general x1, matrix products, per_device(): jnp.einsum('bhtv,btd->hvd', o_heads, grad_out, preferred_element_type=jnp...  75.6 us
  transfers between devices with their start and end apart: 12, of which 1 were waited for; matrix products, arithmetic and copies ran while one was open for 43% of the time, Pallas kernels for 0%

commit v1 on v0

v1 whole, which is shorter than its diff:
```python
import functools

import jax
import jax.numpy as jnp
from jax import lax
from jax.experimental import pallas as pl
from jax.experimental.pallas import tpu as pltpu
from jax.sharding import PartitionSpec as P

EPS = 1e-6
THETA = 10000.0
NEG_BIG = -1e30
LOG2E = 1.4426950408889634
BLOCK_SLOT = (0, 1, 1, 0)
BLOCK_HALF = (0, 0, 1, 1)
F32 = jnp.float32
BF16 = jnp.bfloat16


def layout_positions(seq_local, cp_size, cp_rank):
    half_len = seq_local // 2
    local_idx = jnp.arange(seq_local, dtype=jnp.int32)
    block_id = jnp.where(local_idx < half_len, cp_rank, 2 * cp_size - 1 - cp_rank)
    return block_id * half_len + local_idx % half_len


def rope_tables(positions, rope_dim):
    inv_freq = 1.0 / (THETA ** (jnp.arange(rope_dim // 2, dtype=F32) * 2.0 / rope_dim))
    angles = positions.astype(F32)[:, None] * inv_freq[None, :]
    return jnp.cos(angles), jnp.sin(angles)


def apply_rope(values, cos_tab, sin_tab):
    half_dim = values.shape[-1] // 2
    lead_half = values[..., :half_dim]
    tail_half = values[..., half_dim:]
    return jnp.concatenate([lead_half * cos_tab - tail_half * sin_tab, tail_half * cos_tab + lead_half * sin_tab], axis=-1)


def unrope(grad_vals, cos_tab, sin_tab):
    half_dim = grad_vals.shape[-1] // 2
    lead_half = grad_vals[..., :half_dim]
    tail_half = grad_vals[..., half_dim:]
    return jnp.concatenate([lead_half * cos_tab + tail_half * sin_tab, tail_half * cos_tab - lead_half * sin_tab], axis=-1)


def norm_f32(raw_vals, gain_vec):
    inv_rms = lax.rsqrt(jnp.mean(raw_vals * raw_vals, axis=-1, keepdims=True) + EPS)
    return raw_vals * inv_rms * gain_vec


def dot(lhs, rhs, lhs_dim, rhs_dim):
    return lax.dot_general(lhs, rhs, (((lhs_dim,), (rhs_dim,)), ((), ())), preferred_element_type=F32)


def attn_kernel(scale, n_alias, rank_ref, q_ref, k_ref, v_ref, kp_ref, do0_ref, do1_ref, cos_ref, sin_ref, *rest):
    o_now_ref, o_ref, dq_ref, dk_ref, dv_ref, dkp_ref, kcat, vcat, qcat, dk_acc, dv_acc = rest[n_alias:]
    rank = rank_ref[0]
    blk = q_ref.shape[4] // 2
    nope = k_ref.shape[3]
    qk = q_ref.shape[3]
    half = (qk - nope) // 2
    mid = nope + half

    def where_is(p):
        return jnp.bitwise_xor(rank, BLOCK_SLOT[p]), slice(BLOCK_HALF[p] * blk, BLOCK_HALF[p] * blk + blk)

    for p in range(4):
        slot, rows = where_is(p)
        dst = slice(p * blk, p * blk + blk)
        kcat[dst, :nope] = k_ref[slot, 0, rows, :]
        kcat[dst, nope:] = kp_ref[slot, 0, rows, :]
        vcat[dst, :] = v_ref[slot, 0, rows, :]

    for p in (3, 2, 1, 0):
        slot, rows = where_is(p)
        n_keys = (p + 1) * blk
        cos_p = cos_ref[:, p * blk:p * blk + blk]
        sin_p = sin_ref[:, p * blk:p * blk + blk]
        lead = q_ref[0, slot, 0, nope:mid, rows].astype(F32)
        tail = q_ref[0, slot, 0, mid:, rows].astype(F32)
        qcat[p, :nope, :] = q_ref[0, slot, 0, :nope, rows]
        qcat[p, nope:mid, :] = (lead * cos_p - tail * sin_p).astype(BF16)
        qcat[p, mid:, :] = (tail * cos_p + lead * sin_p).astype(BF16)
        q_blk = qcat[p]
        do_blk = jnp.where(slot == 0, do0_ref[0, 0, :, rows], do1_ref[0, 0, :, rows])
        keys = kcat[:n_keys, :]
        vals = vcat[:n_keys, :]
        st = dot(keys, q_blk, 1, 0)
        key_id = lax.broadcasted_iota(jnp.int32, (blk, blk), 0)
        qry_id = lax.broadcasted_iota(jnp.int32, (blk, blk), 1)
        diag = jnp.where(key_id <= qry_id, st[n_keys - blk:, :], NEG_BIG)
        st = diag if p == 0 else jnp.concatenate([st[:n_keys - blk, :], diag], axis=0)
        col_max = jnp.max(st, axis=0, keepdims=True)
        prob = jnp.exp2((st - col_max) * (scale * LOG2E))
        prob = prob * (1.0 / jnp.sum(prob, axis=0, keepdims=True))
        prob_b = prob.astype(BF16)
        out_blk = dot(vals, prob_b, 0, 0).astype(BF16)
        o_ref[slot, 0, 0, :, rows] = out_blk
        o_now_ref[slot, 0, :, rows] = out_blk
        dpt = dot(vals, do_blk, 1, 0)
        row_dot = jnp.sum(prob * dpt, axis=0, keepdims=True)
        dst_b = (prob * (dpt - row_dot)).astype(BF16)
        dq = dot(keys, dst_b, 0, 0) * scale
        lead = dq[nope:mid, :]
        tail = dq[mid:, :]
        dq_ref[slot, 0, 0, :nope, rows] = dq[:nope, :].astype(BF16)
        dq_ref[slot, 0, 0, nope:mid, rows] = (lead * cos_p + tail * sin_p).astype(BF16)
        dq_ref[slot, 0, 0, mid:, rows] = (tail * cos_p - lead * sin_p).astype(BF16)
        dk_part = dot(dst_b, q_blk, 1, 1)
        dv_part = dot(prob_b, do_blk, 1, 1)
        if p == 3:
            dk_acc[...] = dk_part
            dv_acc[...] = dv_part
        else:
            dk_acc[:n_keys, :] += dk_part
            dv_acc[:n_keys, :] += dv_part

    @pl.when(pl.program_id(0) == 0)
    def _():
        dkp_ref[...] = jnp.zeros_like(dkp_ref)

    for p in range(4):
        slot, rows = where_is(p)
        src = slice(p * blk, p * blk + blk)
        dk_ref[slot, 0, rows, :] = (dk_acc[src, :nope] * scale).astype(BF16)
        dv_ref[slot, 0, rows, :] = dv_acc[src, :].astype(BF16)
        dkp_ref[slot, rows, :] += dk_acc[src, nope:] * scale


def attention(batch, rank, q, k, v, kp, do0, do1, cos_t, sin_t, chain):
    heads, _, n_batch, qk, seq = q.shape
    v_dim = do0.shape[2]
    rope = kp.shape[3]
    nope = qk - rope

    def whole(*shape):
        return pl.BlockSpec(shape, lambda h, r: (0,) * len(shape))

    q_spec = pl.BlockSpec((1, 2, 1, qk, seq), lambda h, r: (h, 0, batch, 0, 0))
    k_spec = pl.BlockSpec((2, 1, seq, nope), lambda h, r: (0, batch, 0, h))
    v_spec = pl.BlockSpec((2, 1, seq, v_dim), lambda h, r: (0, batch, 0, h))
    do_spec = pl.BlockSpec((1, 1, v_dim, seq), lambda h, r: (h, batch, 0, 0))
    o_spec = pl.BlockSpec((2, 1, 1, v_dim, seq), lambda h, r: (0, h, batch, 0, 0))
    dq_spec = pl.BlockSpec((2, 1, 1, qk, seq), lambda h, r: (0, h, batch, 0, 0))
    shared = [jax.ShapeDtypeStruct((2, heads, n_batch, v_dim, seq), BF16), jax.ShapeDtypeStruct((2, heads, n_batch, qk, seq), BF16),
              jax.ShapeDtypeStruct(k.shape, BF16), jax.ShapeDtypeStruct(v.shape, BF16)]
    n_alias = len(chain)
    n_scores = heads * (4 * seq * seq) * 5 // 8
    return pl.pallas_call(
        functools.partial(attn_kernel, qk ** -0.5, n_alias),
        out_shape=[jax.ShapeDtypeStruct((2, heads, v_dim, seq), BF16)] + shared + [jax.ShapeDtypeStruct((2, seq, rope), F32)],
        grid_spec=pltpu.PrefetchScalarGridSpec(
            num_scalar_prefetch=1,
            grid=(heads,),
            in_specs=[q_spec, k_spec, v_spec, pl.BlockSpec((2, 1, seq, rope), lambda h, r: (0, batch, 0, 0)),
                      do_spec, do_spec, whole(rope // 2, 2 * seq), whole(rope // 2, 2 * seq)]
            + [pl.BlockSpec(memory_space=pl.ANY)] * n_alias,
            out_specs=[pl.BlockSpec((2, 1, v_dim, seq), lambda h, r: (0, h, 0, 0)),
                       o_spec, dq_spec, k_spec, v_spec, whole(2, seq, rope)],
            scratch_shapes=[pltpu.VMEM((2 * seq, qk), BF16), pltpu.VMEM((2 * seq, v_dim), BF16),
                            pltpu.VMEM((4, qk, seq // 2), BF16),
                            pltpu.VMEM((2 * seq, qk), F32), pltpu.VMEM((2 * seq, v_dim), F32)],
        ),
        input_output_aliases={9 + i: 1 + i for i in range(n_alias)},
        compiler_params=pltpu.CompilerParams(dimension_semantics=("arbitrary",), vmem_limit_bytes=40 * 2 ** 20),
        cost_estimate=pl.CostEstimate(flops=5 * n_scores * (qk + v_dim), bytes_accessed=heads * seq * 16 * 256, transcendentals=n_scores),
        name="attn_fwd_bwd",
    )(rank, q, k, v, kp, do0, do1, cos_t, sin_t, *chain)


def merge_kernel(rank_ref, mine_ref, other_ref, out_ref):
    is_mine = pl.program_id(0) == rank_ref[0]

    @pl.when(is_mine)
    def _():
        out_ref[...] = mine_ref[...]

    @pl.when(jnp.logical_not(is_mine))
    def _():
        out_ref[...] = other_ref[...]


def merge_halves(rank, mine, other, axis, tile):
    lead, mid, width = mine.shape
    if axis == 0:
        block, steps = (tile, mid, width), lead // tile
        out_map = lambda half, i, r: (half * steps + i, 0, 0)
        out_shape = (2 * lead, mid, width)
    else:
        block, steps = (tile, mid, width), lead // tile
        out_map = lambda half, i, r: (i, half, 0)
        out_shape = (lead, 2 * mid, width)
    last = steps - 1
    mine_map = lambda half, i, r: (jnp.where(half == r[0], i, jnp.where(half == 0, 0, last)), 0, 0)
    other_map = lambda half, i, r: (jnp.where(half != r[0], i, jnp.where(half == 0, 0, last)), 0, 0)
    n_bytes = 4 * mine.size * 4
    return pl.pallas_call(
        merge_kernel,
        out_shape=jax.ShapeDtypeStruct(out_shape, mine.dtype),
        grid_spec=pltpu.PrefetchScalarGridSpec(
            num_scalar_prefetch=1, grid=(2, steps),
            in_specs=[pl.BlockSpec(block, mine_map), pl.BlockSpec(block, other_map)],
            out_specs=pl.BlockSpec(block, out_map)),
        compiler_params=pltpu.CompilerParams(dimension_semantics=("arbitrary", "arbitrary"), vmem_limit_bytes=48 * 2 ** 20),
        cost_estimate=pl.CostEstimate(flops=n_bytes * 100, bytes_accessed=n_bytes, transcendentals=0),
        name="merge_halves",
    )(rank, mine, other)


def down_wgrad_kernel(x0_ref, x1_ref, q0_ref, q1_ref, c0_ref, c1_ref, dq_ref, dc_ref):
    x0 = x0_ref[...]
    x1 = x1_ref[...]
    dq_ref[...] = dot(x0, q0_ref[...], 0, 0) + dot(x1, q1_ref[...], 0, 0)
    dc_ref[...] = dot(c0_ref[...], x0, 0, 0) + dot(c1_ref[...], x1, 0, 0)


def down_wgrad(x0, x1, q0, q1, c0, c1):
    width, q_dim, c_dim = x0.shape[-1], q0.shape[-1], c0.shape[-1]
    operands = [value.reshape(-1, value.shape[-1]) for value in (x0, x1, q0, q1, c0, c1)]
    tokens = operands[0].shape[0]
    tile = min(width, 256)
    x_spec = pl.BlockSpec((tokens, tile), lambda i: (0, i))
    q_spec = pl.BlockSpec((tokens, q_dim), lambda i: (0, 0))
    c_spec = pl.BlockSpec((tokens, c_dim), lambda i: (0, 0))
    grad_q, grad_c = pl.pallas_call(
        down_wgrad_kernel,
        out_shape=[jax.ShapeDtypeStruct((width, q_dim), F32), jax.ShapeDtypeStruct((c_dim, width), F32)],
        grid=(width // tile,),
        in_specs=[x_spec, x_spec, q_spec, q_spec, c_spec, c_spec],
        out_specs=[pl.BlockSpec((tile, q_dim), lambda i: (i, 0)), pl.BlockSpec((c_dim, tile), lambda i: (0, i))],
        compiler_params=pltpu.CompilerParams(dimension_semantics=("arbitrary",), vmem_limit_bytes=56 * 2 ** 20),
        cost_estimate=pl.CostEstimate(flops=4 * tokens * width * (q_dim + c_dim), bytes_accessed=4 * tokens * width + 4 * width * (q_dim + c_dim), transcendentals=0),
        name="down_wgrad",
    )(*operands)
    return grad_q, grad_c.T


def solution(mesh):
    cp_size = mesh.shape['cp']
    tp_size = mesh.shape['tp']
    swap_pairs = [(0, 1), (1, 0)]

    def swap(value):
        return lax.ppermute(value, 'cp', swap_pairs)

    def with_other(value):
        return jnp.stack([value, swap(value)])

    def per_device(hidden, grad_out, w_dq, g_q, w_dkv, g_kv, w_uq, w_uk, w_uv, w_o):
        cp_rank = lax.axis_index('cp')
        tp_rank = lax.axis_index('tp')
        rank = cp_rank.astype(jnp.int32)[None]
        n_batch, seq_local, _ = hidden.shape
        q_lora = w_dq.shape[1]
        kv_lora = g_kv.shape[0]
        nope_dim = w_uk.shape[2]
        v_dim = w_uv.shape[2]
        qk_dim = w_uq.shape[2]
        rope_dim = qk_dim - nope_dim
        heads_core = w_uq.shape[1] // cp_size
        tok_tp = seq_local // tp_size

        positions = layout_positions(seq_local, cp_size, cp_rank)
        cos_tab, sin_tab = rope_tables(positions, rope_dim)
        cos_nat, sin_nat = rope_tables(jnp.arange(cp_size * seq_local, dtype=jnp.int32), rope_dim)
        cos_t, sin_t = cos_nat.T, sin_nat.T

        head0 = cp_rank * heads_core
        uq_mine = lax.dynamic_slice_in_dim(jnp.transpose(w_uq, (1, 2, 0)), head0, heads_core, 0)
        uk_mine = lax.dynamic_slice_in_dim(w_uk, head0, heads_core, 1).reshape(kv_lora, heads_core * nope_dim)
        uv_mine = lax.dynamic_slice_in_dim(w_uv, head0, heads_core, 1).reshape(kv_lora, heads_core * v_dim)
        wo_mine = lax.dynamic_slice_in_dim(w_o, head0, heads_core, 0)

        cq_raw = jnp.einsum('btd,dq->btq', hidden, w_dq, preferred_element_type=F32).astype(BF16)
        kv_raw = jnp.einsum('btd,dc->btc', hidden, w_dkv, preferred_element_type=F32).astype(BF16)
        gq_f32 = g_q.astype(F32)
        gkv_f32 = g_kv.astype(F32)
        c_q = norm_f32(cq_raw.astype(F32), gq_f32).astype(BF16)
        c_kv = norm_f32(kv_raw[..., :kv_lora].astype(F32), gkv_f32).astype(BF16)
        k_pe = apply_rope(kv_raw[..., kv_lora:].astype(F32), cos_tab, sin_tab).astype(BF16)

        c_q2 = with_other(c_q)
        c_kv2 = with_other(c_kv)
        k_pe2 = with_other(k_pe)
        dy_other = swap(grad_out)

        def head_grads(dy):
            return jnp.einsum('hvd,btd->hbvt', wo_mine, dy, preferred_element_type=F32).astype(BF16)

        do0 = head_grads(grad_out)
        do1 = head_grads(dy_other)
        q_all = jnp.einsum('heq,sbtq->hsbet', uq_mine, c_q2, preferred_element_type=F32).astype(BF16)
        k_nope = jnp.einsum('sbtc,cn->sbtn', c_kv2, uk_mine, preferred_element_type=F32).astype(BF16)
        v_heads = jnp.einsum('sbtc,cv->sbtv', c_kv2, uv_mine, preferred_element_type=F32).astype(BF16)

        x_late, q_all = lax.optimization_barrier((hidden, q_all))
        x_other = swap(x_late)

        chain = ()
        dkp_parts = []
        y_parts = []
        for b in range(n_batch):
            res = attention(b, rank, q_all, k_nope, v_heads, k_pe2, do0, do1, cos_t, sin_t, chain)
            o_now, chain, dkp = res[0], tuple(res[1:5]), res[5]
            dkp_parts.append(dkp)
            o_recv = swap(o_now[1])
            o_full = jnp.concatenate([jnp.where(cp_rank == 0, o_now[0], o_recv), jnp.where(cp_rank == 0, o_recv, o_now[0])], axis=0)
            y_b = jnp.einsum('hvt,hvd->td', o_full, w_o, preferred_element_type=F32)
            chain, y_b = lax.optimization_barrier((chain, y_b))
            y_parts.append(lax.psum_scatter(y_b, 'tp', scatter_dimension=0, tiled=True).astype(BF16))
        o_all, dq_all, dk_all, dv_all = chain

        def latent_grads(slot):
            dcq = jnp.einsum('hbet,heq->btq', dq_all[slot], uq_mine, preferred_element_type=F32)
            dckv = jnp.einsum('btn,cn->btc', dk_all[slot], uk_mine, preferred_element_type=F32) + jnp.einsum('btv,cv->btc', dv_all[slot], uv_mine, preferred_element_type=F32)
            return dcq, dckv

        dcq_away, dckv_away = latent_grads(1)
        dcq_home, dckv_home = latent_grads(0)
        dkp2 = jnp.stack(dkp_parts, axis=1)
        latent_part = jnp.concatenate([
            dcq_home + swap(dcq_away),
            dckv_home + swap(dckv_away),
            dkp2[0] + swap(dkp2[1])], axis=-1)
        latent_part, y_parts = lax.optimization_barrier((latent_part, y_parts))
        latent_grad = lax.psum_scatter(latent_part, 'tp', scatter_dimension=1, tiled=True)

        def my_tokens(value, axis):
            return lax.dynamic_slice_in_dim(value, tp_rank * tok_tp, tok_tp, axis)

        cq_mine = my_tokens(cq_raw, 1).astype(F32)
        ckv_mine = my_tokens(kv_raw, 1)[..., :kv_lora].astype(F32)
        grad_cq_raw, grad_g_q = jax.vjp(norm_f32, cq_mine, gq_f32)[1](latent_grad[..., :q_lora])
        grad_ckv_raw, grad_g_kv = jax.vjp(norm_f32, ckv_mine, gkv_f32)[1](latent_grad[..., q_lora:q_lora + kv_lora])
        grad_kpe_raw = unrope(latent_grad[..., q_lora + kv_lora:], my_tokens(cos_tab, 0), my_tokens(sin_tab, 0))
        draw = jnp.concatenate([grad_cq_raw, grad_ckv_raw, grad_kpe_raw], axis=-1).astype(BF16)
        draw = lax.all_gather(draw, 'tp', axis=1, tiled=True)
        grad_g_q, grad_g_kv = lax.psum((grad_g_q, grad_g_kv), ('tp', 'cp'))

        y_stack, draw = lax.optimization_barrier((jnp.stack(y_parts), draw))
        attn_out = lax.all_gather(y_stack, 'tp', axis=1, tiled=True)

        grad_w_o = jnp.einsum('hbvt,btd->hvd', o_all[0], grad_out, preferred_element_type=F32) + jnp.einsum('hbvt,btd->hvd', o_all[1], dy_other, preferred_element_type=F32)
        grad_w_uq = jnp.einsum('shbet,sbtq->heq', dq_all, c_q2, preferred_element_type=F32)
        grad_w_uk = jnp.einsum('sbtc,sbtn->cn', c_kv2, dk_all, preferred_element_type=F32).reshape(kv_lora, heads_core, nope_dim)
        grad_w_uv = jnp.einsum('sbtc,sbtv->cv', c_kv2, dv_all, preferred_element_type=F32).reshape(kv_lora, heads_core, v_dim)
        grad_w_o = merge_halves(rank, grad_w_o, swap(grad_w_o), 0, 1)
        grad_w_uq = jnp.transpose(merge_halves(rank, grad_w_uq, swap(grad_w_uq), 0, 2), (2, 0, 1))
        grad_w_uk = merge_halves(rank, grad_w_uk, swap(grad_w_uk), 1, min(kv_lora, 256))
        grad_w_uv = merge_halves(rank, grad_w_uv, swap(grad_w_uv), 1, min(kv_lora, 256))

        dcq_raw, dkv_raw = lax.optimization_barrier((draw[..., :q_lora], draw[..., q_lora:]))
        dcq_other, dkv_other = swap(dcq_raw), swap(dkv_raw)
        grad_hidden = (jnp.einsum('btq,dq->btd', dcq_raw, w_dq, preferred_element_type=F32) + jnp.einsum('btc,dc->btd', dkv_raw, w_dkv, preferred_element_type=F32)).astype(BF16)
        grad_w_dq, grad_w_dkv = down_wgrad(hidden, x_other, dcq_raw, dcq_other, dkv_raw, dkv_other)
        return (attn_out, grad_hidden, grad_w_dq, grad_g_q, grad_w_dkv, grad_g_kv, grad_w_uq, grad_w_uk, grad_w_uv, grad_w_o)

    seq_spec = P(None, 'cp', None)
    full_spec = P()
    head_spec = P(None, 'tp', None)
    out_head_spec = P('tp', None, None)
    all_specs = (seq_spec, seq_spec, full_spec, full_spec, full_spec, full_spec, head_spec, head_spec, head_spec, out_head_spec)
    return jax.shard_map(per_device, mesh=mesh, in_specs=all_specs, out_specs=all_specs, check_vma=False)
```

time: 2830 us -> 1240 us (0.44)
  blocking collectives: 1040 us -> 23.2 us
  matrix products: 1310 us -> 544 us
  Pallas kernels: 0 us -> 430 us
  local copies, waits for them, and re-layouts: 166 us -> 72.2 us
  waiting for transfers between devices: 178 us -> 98.1 us
  other arithmetic: 104 us -> 45.5 us
    psum x2 -> x1, blocking collectives: 1040 us -> 23.2 us  [per_device(): grad_g_q, grad_g_kv = lax.psum((grad_g_q, grad_g_kv), ('tp', 'cp'))]
    dot_general x36 -> x23, matrix products: 1310 us -> 544 us  [the longest x3 86 us: per_device(): y_b = jnp.einsum('hvt,hvd->td', o_full, w_o, preferred_element_type=F32)]
    pallas_call x0 -> x8, Pallas kernels: none -> 430 us  [the longest x3 244 us: attention(): pl.pallas_call(functools.partial(attn_kernel, qk ** (-0.5), n_alias), out...]
    psum x3 -> x0, waiting for transfers between devices: 178 us -> none  [the longest x1 178 us: per_device(): latent_grad = lax.psum(latent_part, 'tp')]
    unnamed x113 -> x79, local copies, waits for them, and re-layouts: 166 us -> 33.2 us
    reduce_sum x2 -> x0, other arithmetic: 61.8 us -> none  [attend(): row_sum = row_sum * rescale + jnp.sum(prob_blk, axis=-1)]
    all_gather x0 -> x2, waiting for transfers between devices: none -> 52.4 us  [the longest x1 52.4 us: per_device(): draw = lax.all_gather(draw, 'tp', axis=1, tiled=True)]
    reduce_scatter x0 -> x4, waiting for transfers between devices: none -> 38 us  [the longest x1 38 us: per_device(): lax.psum_scatter(latent_part, 'tp', scatter_dimension=1, tiled=True)]
  transfers between devices with their start and end apart: 12 -> 23, of which waited for: 1 -> 4; matrix products, arithmetic and copies ran while one was open for 43% -> 44% of each run, Pallas kernels for 0% -> 28%
where the time goes in v1:
time: 1240 us; the launch traced here: 1230 us
  matrix products  544 us (44%)
  Pallas kernels  430 us (35%)
  waiting for transfers between devices  98.1 us (8%)
  local copies, waits for them, and re-layouts  72.2 us (6%)
  other arithmetic  45.5 us (4%)
  blocking collectives  23.2 us (2%)
  between operations  15 us (1%)
    pallas_call x3, Pallas kernels, attention(): pl.pallas_call(functools.partial(attn_kernel, qk ** (-0.5), n_alias), out...  244 us
    pallas_call x4, Pallas kernels, merge_halves(): pl.pallas_call(merge_kernel, out_shape=jax.ShapeDtypeStruct(out_shape, mi...  108 us
    dot_general x3, matrix products, per_device(): y_b = jnp.einsum('hvt,hvd->td', o_full, w_o, preferred_element_type=F32)  86 us
    dot_general x2, matrix products, head_grads(): jnp.einsum('hvd,btd->hbvt', wo_mine, dy, preferred_element_type=F32)  82.8 us
    pallas_call x1, Pallas kernels, down_wgrad(): pl.pallas_call(down_wgrad_kernel, out_shape=[jax.ShapeDtypeStruct((width,...  77.7 us
    all_gather x1, waiting for transfers between devices, per_device(): draw = lax.all_gather(draw, 'tp', axis=1, tiled=True)  52.4 us
    dot_general x1, matrix products, per_device(): jnp.einsum('hbvt,btd->hvd', o_all[1], dy_other, preferred_element_type=F32)  44.8 us
    dot_general x2, matrix products, latent_grads(): jnp.einsum('hbet,heq->btq', dq_all[slot], uq_mine, preferred_element_type...  44 us
  transfers between devices with their start and end apart: 23, of which 4 were waited for; matrix products, arithmetic and copies ran while one was open for 44% of the time, Pallas kernels for 28%

profile of v1, /device:TPU:0, one launch (start us, length us, event | category | flops | bytes accessed | tf_op | source)
XLA Modules:
  0.0 1233.8 jit_solution(1358846044211652258)
XLA Ops:
  7.3 17.1 %fusion.110 = bf16[3,512,576]{2,1,0:T(8,128)(2,1)S(1)} fusion(bf16[3,512,5120]{2,1,0:T(8,128)(2,1)} %param.10, bf16[5120,576]{0,1:T(8,128)(2,1)} %param.14), kind=kOutput, calls=%fused_computation.117 | convolution fusion | flops 9060581376 | bytes 23396352 | tf_op jit(solution)/shard_map/btd,dc->btc/dot_general | solution.py:276
  29.4 32.0 %fusion.19 = (f32[3,512]{1,0:T(4,128)S(1)}, bf16[3,512,1536]{2,1,0:T(8,128)(2,1)S(1)}) fusion(bf16[3,512,5120]{2,1,0:T(8,128)(2,1)} %param.10, bf16[5120,1536]{1,0:T(8,128)(2,1)} %param.12), kind=kOutput, calls=%fused_computation.25 | convolution fusion | flops 24168626176 | bytes 36182016 | tf_op jit(solution)/shard_map/btd,dq->btq/dot_general | solution.py:275
  65.6 41.5 %convert_bitcast_fusion.2.do0_ref = bf16[16,3,128,512]{3,2,1,0:T(8,128)(2,1)} fusion(bf16[3,512,5120]{2,1,0:T(8,128)(2,1)} %param.11, bf16[32,128,5120]{2,1,0:T(8,128)(2,1)} %param.19, s32[]{:T(128)S(6)} %select_n.59), kind=kOutput, calls=%fused_computation.68 | convolution fusion | flops 32215400448 | bytes 42991620 | tf_op jit(solution)/shard_map/hvd,btd->hbvt/dot_general | solution.py:289
  126.5 11.9 convolution_convert_fusion.v_ref
  138.4 11.3 convolution_convert_fusion.1.k_ref
  149.6 35.0 %convert_bitcast_fusion.q_ref = bf16[16,2,3,192,512]{4,3,2,1,0:T(8,128)(2,1)} fusion(bf16[1536,32,192]{0,2,1:T(8,128)(2,1)} %param.16, s32[]{:T(128)S(6)} %select_n.59, bf16[1,3,512,1536]{3,2,1,0:T(8,128)(2,1)} %bitcast.3, bf16[1,3,512,1536]{3,2,1,0:T(8,128)(2,1)S(1)} %fusion.154), kind=kOutput, calls=%fused_computation.6 | convolution fusion | flops 29019340800 | bytes 37748740 | tf_op jit(solution)/shard_map/heq,sbtq->hsbet/dot_general | solution.py:293
  184.7 41.3 %convert_bitcast_fusion.1.do1_ref = bf16[16,3,128,512]{3,2,1,0:T(8,128)(2,1)} fusion(bf16[3,512,5120]{2,1,0:T(8,128)(2,1)} %collective-permute-done.3, bf16[32,128,5120]{2,1,0:T(8,128)(2,1)} %param.19, s32[]{:T(128)S(6)} %select_n.59), kind=kOutput, calls=%fused_computation.67 | convolution fusion | flops 32215400448 | bytes 42991620 | tf_op jit(solution)/shard_map/hvd,btd->hbvt/dot_general | solution.py:289
  228.8 81.4 %attn_fwd_bwd.3 = (bf16[2,16,128,512]{3,2,1,0:T(8,128)(2,1)S(1)}, bf16[2,16,3,128,512]{4,3,2,1,0:T(8,128)(2,1)}, bf16[2,16,3,192,512]{4,3,2,1,0:T(8,128)(2,1)}, ...) custom-call(s32[1]{0:T(128)} %bitcast.rank_ref, ...), custom_call_target="tpu_custom_call" | custom-call | flops 16777216000 | bytes 33554432 | tf_op jit(solution)/shard_map/attn_fwd_bwd/pallas_call | solution.py:150
  320.5 28.7 %convolution_bitcast_fusion.2 = f32[512,5120]{1,0:T(8,128)} fusion(bf16[32,128,5120]{2,1,0:T(8,128)(2,1)} %param.19, bf16[16,128,512]{2,1,0:T(8,128)(2,1)S(1)} %get-tuple-element.111, bf16[16,128,512]{2,1,0:T(8,128)(2,1)S(1)} %get-tuple-element.110), kind=kOutput, calls=%fused_computation.45 | convolution fusion | flops 21476933632 | bytes 56623104 | tf_op jit(solution)/shard_map/hvt,hvd->td/dot_general | solution.py:309
  352.0 81.2 %attn_fwd_bwd.4 = (bf16[2,16,128,512]{3,2,1,0:T(8,128)(2,1)S(1)}, bf16[2,16,3,128,512]{4,3,2,1,0:T(8,128)(2,1)}, bf16[2,16,3,192,512]{4,3,2,1,0:T(8,128)(2,1)}, ...) custom-call(s32[1]{0:T(128)} %bitcast.rank_ref, ...), custom_call_target="tpu_custom_call", output_to_operand_aliasing={{1}: (9, {}), {2}: (10, {}), {3}: (11, {}), {4}: (12, {})} | custom-call | flops 16777216000 | bytes 33554432 | tf_op jit(solution)/shard_map/attn_fwd_bwd/pallas_call | solution.py:150
  437.9 28.7 %convolution_bitcast_fusion.1 = f32[512,5120]{1,0:T(8,128)} fusion(bf16[32,128,5120]{2,1,0:T(8,128)(2,1)} %param.19, bf16[16,128,512]{2,1,0:T(8,128)(2,1)S(1)} %get-tuple-element.109, bf16[16,128,512]{2,1,0:T(8,128)(2,1)S(1)} %get-tuple-element.108), kind=kOutput, calls=%fused_computation.44 | convolution fusion | flops 21476933632 | bytes 56623104 | tf_op jit(solution)/shard_map/hvt,hvd->td/dot_general | solution.py:309
  469.5 81.3 %attn_fwd_bwd.5 = (bf16[2,16,128,512]{3,2,1,0:T(8,128)(2,1)S(1)}, bf16[2,16,3,128,512]{4,3,2,1,0:T(8,128)(2,1)}, bf16[2,16,3,192,512]{4,3,2,1,0:T(8,128)(2,1)}, ...) custom-call(s32[1]{0:T(128)} %bitcast.rank_ref, ...), custom_call_target="tpu_custom_call", output_to_operand_aliasing={{1}: (9, {}), {2}: (10, {}), {3}: (11, {}), {4}: (12, {})} | custom-call | flops 16777216000 | bytes 33554432 | tf_op jit(solution)/shard_map/attn_fwd_bwd/pallas_call | solution.py:150
  567.8 28.6 %convolution_bitcast_fusion = f32[512,5120]{1,0:T(8,128)} fusion(bf16[32,128,5120]{2,1,0:T(8,128)(2,1)} %param.19, bf16[16,128,512]{2,1,0:T(8,128)(2,1)S(1)} %get-tuple-element.107, bf16[16,128,512]{2,1,0:T(8,128)(2,1)S(1)} %get-tuple-element.106), kind=kOutput, calls=%fused_computation.43 | convolution fusion | flops 21476933632 | bytes 56623104 | tf_op jit(solution)/shard_map/hvt,hvd->td/dot_general | solution.py:309
  596.5 22.2 %fusion.63 = f32[3,512,1536]{2,1,0:T(8,128)} fusion(bf16[1536,32,192]{0,2,1:T(8,128)(2,1)} %param.16, s32[]{:T(128)S(6)} %select_n.59, bf16[2,16,3,192,512]{4,3,2,1,0:T(8,128)(2,1)} %get-tuple-element.79), kind=kOutput, calls=%fused_computation.72 | convolution fusion | flops 14495514624 | bytes 28311556 | tf_op jit(solution)/shard_map/hbet,heq->btq/dot_general | solution.py:315
  624.7 8.2 fusion.115
  633.2 39.1 %fusion.8 = f32[16,128,5120,1]{2,1,3,0:T(8,128)} fusion(bf16[3,512,5120]{2,1,0:T(8,128)(2,1)} %param.11, bf16[2,16,3,128,512]{4,3,2,1,0:T(8,128)(2,1)S(1)} %bitcast.209), kind=kOutput, calls=%fused_computation.11 | convolution fusion | flops 32212254720 | bytes 63963136 | tf_op jit(solution)/shard_map/hbvt,btd->hvd/dot_general | solution.py:344
  677.8 7.5 add_add_fusion.1
  685.4 21.8 %bitcast_add_fusion.1 = f32[3,512,1536]{2,1,0:T(8,128)S(1)} fusion(f32[3,512,1536]{2,1,0:T(8,128)} %collective-permute-done.7, bf16[1536,32,192]{0,2,1:T(8,128)(2,1)} %param.16, s32[]{:T(128)S(6)} %select_n.59, bf16[2,16,3,192,512]{4,3,2,1,0:T(8,128)(2,1)} %get-tuple-element.79), kind=kOutput, calls=%fused_computation.37 | convolution fusion | flops 14497873920 | bytes 37748740 | tf_op jit(solution)/shard_map/hbet,heq->btq/dot_general | solution.py:315
  721.4 44.8 %bitcast_add_fusion.mine_ref = f32[16,128,5120]{2,1,0:T(8,128)} fusion(f32[16,128,5120,1]{2,1,3,0:T(8,128)} %fusion.8, bf16[3,512,5120]{2,1,0:T(8,128)(2,1)} %collective-permute-done.3, bf16[2,16,3,128,512]{4,3,2,1,0:T(8,128)(2,1)} %get-tuple-element.99), kind=kOutput, calls=%fused_computation | convolution fusion | flops 32222740480 | bytes 105906176 | tf_op jit(solution)/shard_map/hbvt,btd->hvd/dot_general | solution.py:344
  766.4 37.5 %fusion.34.mine_ref = f32[16,192,1536]{2,1,0:T(8,128)} fusion(bf16[2,16,3,192,512]{4,3,2,1,0:T(8,128)(2,1)} %get-tuple-element.79, bf16[1,3,512,1536]{3,2,1,0:T(8,128)(2,1)} %bitcast.3, bf16[1,3,512,1536]{3,2,1,0:T(8,128)(2,1)} %copy-done.15), kind=kOutput, calls=%fused_computation.42 | convolution fusion | flops 28995747840 | bytes 47185920 | tf_op jit(solution)/shard_map/shbet,sbtq->heq/dot_general | solution.py:345
  806.9 38.0 %reduce-scatter.11.cloned.1.call-done = f32[3,128,2112]{2,1,0:T(8,128)} async-done(((f32[3,512,2112]{2,1,0:T(8,128)}), f32[3,128,2112]{2,1,0:T(8,128)}) %reduce-scatter.11.cloned.1.call-update) | async-done | bytes 3244048 | tf_op jit(solution)/shard_map/reduce_scatter | solution.py:327
  853.6 10.1 fusion.103
  869.0 52.4 %all-gather.3.cloned.1.call-done = bf16[3,512,2112]{2,1,0:T(8,128)(2,1)} async-done(((bf16[3,128,2112]{2,1,0:T(8,128)(2,1)}), bf16[3,512,2112]{2,1,0:T(8,128)(2,1)}) %all-gather.3.cloned.1.call-update) | async-done | bytes 6488080 | tf_op jit(solution)/shard_map/all_gather | solution.py:338
  921.4 10.1 fusion.98
  932.9 7.5 merge_halves.6
  949.4 30.1 %merge_halves.4 = f32[32,192,1536]{2,1,0:T(8,128)} custom-call(s32[1]{0:T(128)} %bitcast.rank_ref, f32[16,192,1536]{2,1,0:T(8,128)} %fusion.34.mine_ref, f32[16,192,1536]{2,1,0:T(8,128)} %collective-permute-done.13.other_ref), custom_call_target="tpu_custom_call" | custom-call | flops 7549747200 | bytes 75497472 | tf_op jit(solution)/shard_map/merge_halves/pallas_call | solution.py:198
  979.5 64.0 %merge_halves.7 = f32[32,128,5120]{2,1,0:T(8,128)} custom-call(s32[1]{0:T(128)} %bitcast.rank_ref, f32[16,128,5120]{2,1,0:T(8,128)} %bitcast_add_fusion.mine_ref, f32[16,128,5120]{2,1,0:T(8,128)} %collective-permute-done.16.other_ref), custom_call_target="tpu_custom_call" | custom-call | flops 16777216000 | bytes 167772160 | tf_op jit(solution)/shard_map/merge_halves/pallas_call | solution.py:198
  1043.4 23.2 %all-reduce = (f32[1536]{0:T(1024)}, f32[512]{0:T(512)}) all-reduce(f32[1536]{0:T(1024)S(1)} %get-tuple-element.100, f32[512]{0:T(512)S(1)} %get-tuple-element.102), channel_id=1, replica_groups=mesh['tp'=4,'cp'=2] {'tp','cp'}, use_global_device_ids=true, to_apply=%region_11.12 | all-reduce | flops 2048 | bytes 16384 | tf_op jit(solution)/shard_map/psum | solution.py:339
  1073.6 31.9 %fusion.11 = f32[3,512,5120]{2,1,0:T(8,128)} fusion(bf16[3,512,1536]{2,1,0:T(8,128)(2,1)} %slice.110, bf16[5120,1536]{1,0:T(8,128)(2,1)} %param.12), kind=kOutput, calls=%fused_computation.14 | convolution fusion | flops 24159191040 | bytes 51904512 | tf_op jit(solution)/shard_map/btq,dq->btd/dot_general | solution.py:355
  1108.1 23.9 %add_convert_fusion = bf16[3,512,5120]{2,1,0:T(8,128)(2,1)} fusion(f32[3,512,5120]{2,1,0:T(8,128)} %fusion.11, bf16[3,512,576]{2,1,0:T(8,128)(2,1)S(1)} %slice.111, bf16[5120,576]{0,1:T(8,128)(2,1)} %param.14), kind=kOutput, calls=%fused_computation.1 | convolution fusion | flops 9075425280 | bytes 54853632 | tf_op jit(solution)/shard_map/btc,dc->btd/dot_general | solution.py:355
  1135.9 77.7 %down_wgrad.1 = (f32[5120,1536]{1,0:T(8,128)}, f32[576,5120]{1,0:T(8,128)}) custom-call(bf16[1536,5120]{1,0:T(8,128)(2,1)} %bitcast.219, bf16[1536,5120]{1,0:T(8,128)(2,1)} %bitcast.54.x1_ref, bf16[1536,1536]{1,0:T(8,128)(2,1)} %bitcast.55.q0_ref, bf16[1536,1536]{1,0:T(8,128)(2,1)} %bitcast.56.q1_ref, bf16[1536,576]{1,0:T(8,128)(2,1)} %bitcast.211, ...), custom_call_target="tpu_custom_call" | custom-call | flops 66437775360 | bytes 74711040 | tf_op jit(solution)/shard_map/down_wgrad/pallas_call | solution.py:226
  1213.6 13.2 %copy.119 = bf16[3,512,5120]{2,1,0:T(8,128)(2,1)} copy(bf16[3,512,5120]{2,1,0:T(8,128)(2,1)} %all-gather.5.cloned.1.call-done) | data formatting | bytes 31457280
  (188 shorter events, 135.8 us)
Async XLA Ops:
  7.2 705.2 %reduce-scatter.5.cloned.1.call-start = ((), (), s32[]{:S(2)}) async-start(), calls=%async_computation.4 | async-start | bytes 13107200 | tf_op jit(solution)/shard_map/reduce_scatter | solution.py:311
  24.3 96.0 %copy-start.6 = (bf16[3,512,576]{2,1,0:T(8,128)(2,1)}, bf16[3,512,576]{2,1,0:T(8,128)(2,1)S(1)}, u32[]{:S(2)}) copy-start(bf16[3,512,576]{2,1,0:T(8,128)(2,1)S(1)} %fusion.110) | copy-start | bytes 5308420
  26.5 99.7 %collective-permute-start.2 = (bf16[3,512,64]{2,1,0:T(8,128)(2,1)S(1)}, bf16[3,512,64]{2,1,0:T(8,128)(2,1)S(1)}, u32[]{:S(2)}, u32[]{:S(2)}) collective-permute-start(bf16[3,512,64]{2,1,0:T(8,128)(2,1)S(1)} %pad_maximum_fusion.8), channel_id=1, source_target_pairs={{0,1},{1,0},{2,3},{3,2},{4,5},{5,4},{6,7},{7,6}} | collective-permute-start | bytes 589832 | tf_op jit(solution)/shard_map/ppermute | solution.py:245
  29.3 32.0 %copy-start.31 = (bf16[1536]{0:T(1024)(128)(2,1)S(1)}, bf16[1536]{0:T(1024)(128)(2,1)}, u32[]{:S(2)}) copy-start(bf16[1536]{0:T(1024)(128)(2,1)} %param.13) | copy-start | bytes 9220
  29.3 97.1 %collective-permute-start.1 = (bf16[3,512,512]{2,1,0:T(8,128)(2,1)}, bf16[3,512,512]{2,1,0:T(8,128)(2,1)}, u32[]{:S(2)}, u32[]{:S(2)}) collective-permute-start(bf16[3,512,512]{2,1,0:T(8,128)(2,1)} %fusion.90), channel_id=1, source_target_pairs={{0,1},{1,0},{2,3},{3,2},{4,5},{5,4},{6,7},{7,6}} | collective-permute-start | bytes 4718600 | tf_op jit(solution)/shard_map/ppermute | solution.py:245
  61.4 60.1 %copy-start.26 = (f32[1536]{0:T(1024)}, f32[1536]{0:T(1024)S(1)}, u32[]{:S(2)}) copy-start(f32[1536]{0:T(1024)S(1)} %convert_element_type.102) | copy-start | bytes 18436
  65.1 84.5 %collective-permute-start = (bf16[3,512,1536]{2,1,0:T(8,128)(2,1)}, bf16[3,512,1536]{2,1,0:T(8,128)(2,1)}, u32[]{:S(2)}, u32[]{:S(2)}) collective-permute-start(bf16[3,512,1536]{2,1,0:T(8,128)(2,1)} %fusion.21), channel_id=1, source_target_pairs={{0,1},{1,0},{2,3},{3,2},{4,5},{5,4},{6,7},{7,6}} | collective-permute-start | bytes 14155784 | tf_op jit(solution)/shard_map/ppermute | solution.py:245
  65.6 119.1 %collective-permute-start.3 = (bf16[3,512,5120]{2,1,0:T(8,128)(2,1)}, bf16[3,512,5120]{2,1,0:T(8,128)(2,1)}, u32[]{:S(2)}, u32[]{:S(2)}) collective-permute-start(bf16[3,512,5120]{2,1,0:T(8,128)(2,1)} %param.11), channel_id=1, source_target_pairs={{0,1},{1,0},{2,3},{3,2},{4,5},{5,4},{6,7},{7,6}} | collective-permute-start | bytes 47185928 | tf_op jit(solution)/shard_map/ppermute | solution.py:245
  125.6 24.0 %copy-start.15 = (bf16[1,3,512,1536]{3,2,1,0:T(8,128)(2,1)}, bf16[1,3,512,1536]{3,2,1,0:T(8,128)(2,1)S(1)}, u32[]{:S(2)}) copy-start(bf16[1,3,512,1536]{3,2,1,0:T(8,128)(2,1)S(1)} %fusion.154) | copy-start | bytes 14155780
  313.7 4.3 collective-permute-start.4
  349.2 366.2 %reduce-scatter.7.cloned.1.call-start = ((), (), s32[]{:S(2)}) async-start(), calls=%async_computation.5 | async-start | bytes 13107200 | tf_op jit(solution)/shard_map/reduce_scatter | solution.py:311
  433.4 4.2 collective-permute-start.5
  466.6 251.7 %reduce-scatter.9.cloned.1.call-start = ((), (), s32[]{:S(2)}) async-start(), calls=%async_computation.6 | async-start | bytes 13107200 | tf_op jit(solution)/shard_map/reduce_scatter | solution.py:311
  554.3 11.0 collective-permute-start.6
  556.2 6.7 collective-permute-start.9
  596.4 22.5 %copy-start.19 = (bf16[512,2048,1]{1,0,2:T(8,128)(2,1)S(1)}, bf16[512,2048,1]{1,0,2:T(8,128)(2,1)}, u32[]{:S(2)}) copy-start(bf16[512,2048,1]{1,0,2:T(8,128)(2,1)} %reshape.245) | copy-start | bytes 6291460
  596.4 248.5 %reduce-scatter.11.cloned.1.call-start = ((), (), s32[]{:S(2)}) async-start(), calls=%async_computation.7 | async-start | bytes 16711680 | tf_op jit(solution)/shard_map/reduce_scatter | solution.py:327
  618.7 66.7 %collective-permute-start.7 = (f32[3,512,1536]{2,1,0:T(8,128)}, f32[3,512,1536]{2,1,0:T(8,128)}, u32[]{:S(2)}, u32[]{:S(2)}) collective-permute-start(f32[3,512,1536]{2,1,0:T(8,128)} %fusion.63), channel_id=1, source_target_pairs={{0,1},{1,0},{2,3},{3,2},{4,5},{5,4},{6,7},{7,6}} | collective-permute-start | bytes 28311560 | tf_op jit(solution)/shard_map/ppermute | solution.py:245
  632.8 45.0 %collective-permute-start.8 = (f32[3,512,512]{2,1,0:T(8,128)}, f32[3,512,512]{2,1,0:T(8,128)}, u32[]{:S(2)}, u32[]{:S(2)}) collective-permute-start(f32[3,512,512]{2,1,0:T(8,128)} %fusion.115), channel_id=1, source_target_pairs={{0,1},{1,0},{2,3},{3,2},{4,5},{5,4},{6,7},{7,6}} | collective-permute-start | bytes 9437192 | tf_op jit(solution)/shard_map/ppermute | solution.py:245
  721.3 200.0 %all-gather.3.cloned.1.call-start = ((), (), s32[]{:S(2)}) async-start(), calls=%async_computation.8 | async-start | bytes 8355840 | tf_op jit(solution)/shard_map/all_gather | solution.py:338
  766.1 38.1 %copy-start.7 = (bf16[3,512,576]{2,1,0:T(8,128)(2,1)S(1)}, bf16[3,512,576]{2,1,0:T(8,128)(2,1)}, u32[]{:S(2)}) copy-start(bf16[3,512,576]{2,1,0:T(8,128)(2,1)} %copy-done.6) | copy-start | bytes 5308420
  766.1 78.7 %copy-start.30 = (f32[512]{0:T(512)S(1)}, f32[512]{0:T(512)}, u32[]{:S(2)}) copy-start(f32[512]{0:T(512)} %copy-done.29) | copy-start | bytes 6148
  766.1 80.4 %copy-start.27 = (f32[1536]{0:T(1024)S(1)}, f32[1536]{0:T(1024)}, u32[]{:S(2)}) copy-start(f32[1536]{0:T(1024)} %copy-done.26) | copy-start | bytes 18436
  766.1 213.3 %collective-permute-start.16 = (f32[16,128,5120]{2,1,0:T(8,128)}, f32[16,128,5120]{2,1,0:T(8,128)}, u32[]{:S(2)}, u32[]{:S(2)}) collective-permute-start(f32[16,128,5120]{2,1,0:T(8,128)} %bitcast_add_fusion.mine_ref), channel_id=1, source_target_pairs={{0,1},{1,0},{2,3},{3,2},{4,5},{5,4},{6,7},{7,6}} | collective-permute-start | bytes 125829128 | tf_op jit(solution)/shard_map/ppermute | solution.py:245
  803.8 145.5 %collective-permute-start.13 = (f32[16,192,1536]{2,1,0:T(8,128)}, f32[16,192,1536]{2,1,0:T(8,128)}, u32[]{:S(2)}, u32[]{:S(2)}) collective-permute-start(f32[16,192,1536]{2,1,0:T(8,128)} %fusion.34.mine_ref), channel_id=1, source_target_pairs={{0,1},{1,0},{2,3},{3,2},{4,5},{5,4},{6,7},{7,6}} | collective-permute-start | bytes 56623112 | tf_op jit(solution)/shard_map/ppermute | solution.py:245
  853.6 360.0 %all-gather.5.cloned.1.call-start = ((), (), s32[]{:S(2)}) async-start(), calls=%async_computation.9 | async-start | bytes 19660800 | tf_op jit(solution)/shard_map/all_gather | solution.py:342
  866.7 66.2 %collective-permute-start.15 = (f32[512,16,128]{2,1,0:T(8,128)}, f32[512,16,128]{2,1,0:T(8,128)}, u32[]{:S(2)}, u32[]{:S(2)}) collective-permute-start(f32[512,16,128]{2,1,0:T(8,128)} %bitcast.84.mine_ref), channel_id=1, source_target_pairs={{0,1},{1,0},{2,3},{3,2},{4,5},{5,4},{6,7},{7,6}} | collective-permute-start | bytes 12582920 | tf_op jit(solution)/shard_map/ppermute | solution.py:245
  932.4 8.1 collective-permute-start.14
  932.4 203.4 %collective-permute-start.10 = (bf16[3,512,5120]{2,1,0:T(8,128)(2,1)}, bf16[3,512,5120]{2,1,0:T(8,128)(2,1)}, u32[]{:S(2)}, u32[]{:S(2)}) collective-permute-start(bf16[3,512,5120]{2,1,0:T(8,128)(2,1)} %param.10), channel_id=1, source_target_pairs={{0,1},{1,0},{2,3},{3,2},{4,5},{5,4},{6,7},{7,6}} | collective-permute-start | bytes 47185928 | tf_op jit(solution)/shard_map/ppermute | solution.py:245
  1073.2 34.8 %copy-start.10 = (bf16[3,512,576]{2,1,0:T(8,128)(2,1)}, bf16[3,512,576]{2,1,0:T(8,128)(2,1)S(1)}, u32[]{:S(2)}) copy-start(bf16[3,512,576]{2,1,0:T(8,128)(2,1)S(1)} %slice.111) | copy-start | bytes 5308420
  1073.2 62.6 %collective-permute-start.11 = (bf16[3,512,1536]{2,1,0:T(8,128)(2,1)}, bf16[3,512,1536]{2,1,0:T(8,128)(2,1)}, u32[]{:S(2)}, u32[]{:S(2)}) collective-permute-start(bf16[3,512,1536]{2,1,0:T(8,128)(2,1)} %slice.110), channel_id=1, source_target_pairs={{0,1},{1,0},{2,3},{3,2},{4,5},{5,4},{6,7},{7,6}} | collective-permute-start | bytes 14155784 | tf_op jit(solution)/shard_map/ppermute | solution.py:245
  1107.7 24.3 %collective-permute-start.12 = (bf16[3,512,576]{1,2,0:T(8,128)(2,1)}, bf16[3,512,576]{1,2,0:T(8,128)(2,1)}, u32[]{:S(2)}, u32[]{:S(2)}) collective-permute-start(bf16[3,512,576]{1,2,0:T(8,128)(2,1)} %copy.56), channel_id=1, source_target_pairs={{0,1},{1,0},{2,3},{3,2},{4,5},{5,4},{6,7},{7,6}} | collective-permute-start | bytes 5308424 | tf_op jit(solution)/shard_map/ppermute | solution.py:245
  (29 other events, 171.4 us)
Sparse Core Ops, SparseCore 0:
  349.3 99.9 reduce-scatter.4
  466.8 99.9 reduce-scatter.6
  596.5 99.8 reduce-scatter.8
  721.4 123.4 reduce-scatter.10
  853.7 67.5 all-gather.2
  922.9 144.4 all-gather.4

commit v2 on v1

--- a/solution.py
+++ b/solution.py
@@ -6,6 +6,7 @@
 from jax.experimental import pallas as pl
 from jax.experimental.pallas import tpu as pltpu
 from jax.sharding import PartitionSpec as P
+
 
 EPS = 1e-6
 THETA = 10000.0
@@ -54,78 +55,124 @@
 
 
 def attn_kernel(scale, n_alias, rank_ref, q_ref, k_ref, v_ref, kp_ref, do0_ref, do1_ref, cos_ref, sin_ref, *rest):
-    o_now_ref, o_ref, dq_ref, dk_ref, dv_ref, dkp_ref, kcat, vcat, qcat, dk_acc, dv_acc = rest[n_alias:]
+    o_now_ref, o_ref, dq_ref, dk_ref, dv_ref, dkp_ref, kcat, k_t, v_t, qcat, dk_acc, dv_acc, score, prob_b, grad_s = rest[n_alias:]
     rank = rank_ref[0]
     blk = q_ref.shape[4] // 2
     nope = k_ref.shape[3]
     qk = q_ref.shape[3]
     half = (qk - nope) // 2
     mid = nope + half
-
-    def where_is(p):
-        return jnp.bitwise_xor(rank, BLOCK_SLOT[p]), slice(BLOCK_HALF[p] * blk, BLOCK_HALF[p] * blk + blk)
+    place = [(jnp.bitwise_xor(rank, BLOCK_SLOT[p]), slice(BLOCK_HALF[p] * blk, BLOCK_HALF[p] * blk + blk)) for p in range(4)]
+
+    def span(p):
+        return slice(p * blk, p * blk + blk)
+
+    @pl.when(pl.program_id(0) == 0)
+    def _():
+        dkp_ref[...] = jnp.zeros_like(dkp_ref)
+        for p in range(4):
+            slot, rows = place[p]
+            k_rope = kp_ref[slot, 0, rows, :]
+            kcat[span(p), nope:] = k_rope
+            k_t[nope:, span(p)] = k_rope.T
 
     for p in range(4):
-        slot, rows = where_is(p)
-        dst = slice(p * blk, p * blk + blk)
-        kcat[dst, :nope] = k_ref[slot, 0, rows, :]
-        kcat[dst, nope:] = kp_ref[slot, 0, rows, :]
-        vcat[dst, :] = v_ref[slot, 0, rows, :]
-
-    for p in (3, 2, 1, 0):
-        slot, rows = where_is(p)
-        n_keys = (p + 1) * blk
-        cos_p = cos_ref[:, p * blk:p * blk + blk]
-        sin_p = sin_ref[:, p * blk:p * blk + blk]
+        slot, rows = place[p]
+        k_blk = k_ref[slot, 0, rows, :]
+        kcat[span(p), :nope] = k_blk
+        k_t[:nope, span(p)] = k_blk.T
+        v_t[:, span(p)] = v_ref[slot, 0, rows, :].T
+
+    untouched = [True] * 4
+    pending = [4 - j for j in range(4)]
+
+    def flush(j):
+        slot, rows = place[j]
+        dk_ref[slot, 0, rows, :] = (dk_acc[span(j), :nope] * scale).astype(BF16)
+        dv_ref[slot, 0, rows, :] = dv_acc[span(j), :].astype(BF16)
+        dkp_ref[slot, rows, :] += dk_acc[span(j), nope:] * scale
+
+    def steps(p, buf):
+        slot, rows = place[p]
+        n_blk = p + 1
+        yield False, 0
+        cos_p = cos_ref[:, span(p)]
+        sin_p = sin_ref[:, span(p)]
         lead = q_ref[0, slot, 0, nope:mid, rows].astype(F32)
         tail = q_ref[0, slot, 0, mid:, rows].astype(F32)
         qcat[p, :nope, :] = q_ref[0, slot, 0, :nope, rows]
         qcat[p, nope:mid, :] = (lead * cos_p - tail * sin_p).astype(BF16)
         qcat[p, mid:, :] = (tail * cos_p + lead * sin_p).astype(BF16)
-        q_blk = qcat[p]
+        col_max = None
+        for j in range(n_blk):
+            yield True, 2
+            st = dot(kcat[span(j), :], qcat[p], 1, 0)
+            if j == p:
+                key_id = lax.broadcasted_iota(jnp.int32, (blk, blk), 0)
+                qry_id = lax.broadcasted_iota(jnp.int32, (blk, blk), 1)
+                st = jnp.where(key_id <= qry_id, st, NEG_BIG)
+            score[buf, span(j), :] = st
+            part = jnp.max(st, axis=0, keepdims=True)
+            col_max = part if col_max is None else jnp.maximum(col_max, part)
+        col_sum = None
+        for j in range(n_blk):
+            yield False, 3
+            prob = jnp.exp2((score[buf, span(j), :] - col_max) * (scale * LOG2E))
+            score[buf, span(j), :] = prob
+            part = jnp.sum(prob, axis=0, keepdims=True)
+            col_sum = part if col_sum is None else col_sum + part
+        inv_sum = 1.0 / col_sum
+        for j in range(n_blk):
+            yield False, 2
+            prob_b[buf, span(j), :] = (score[buf, span(j), :] * inv_sum).astype(BF16)
+        n_keys = n_blk * blk
+        yield True, n_blk
+        out = dot(v_t[:, :n_keys], prob_b[buf, :n_keys, :], 1, 0)
+        out_b = out.astype(BF16)
+        o_ref[slot, 0, 0, :, rows] = out_b
+        o_now_ref[slot, 0, :, rows] = out_b
         do_blk = jnp.where(slot == 0, do0_ref[0, 0, :, rows], do1_ref[0, 0, :, rows])
-        keys = kcat[:n_keys, :]
-        vals = vcat[:n_keys, :]
-        st = dot(keys, q_blk, 1, 0)
-        key_id = lax.broadcasted_iota(jnp.int32, (blk, blk), 0)
-        qry_id = lax.broadcasted_iota(jnp.int32, (blk, blk), 1)
-        diag = jnp.where(key_id <= qry_id, st[n_keys - blk:, :], NEG_BIG)
-        st = diag if p == 0 else jnp.concatenate([st[:n_keys - blk, :], diag], axis=0)
-        col_max = jnp.max(st, axis=0, keepdims=True)
-        prob = jnp.exp2((st - col_max) * (scale * LOG2E))
-        prob = prob * (1.0 / jnp.sum(prob, axis=0, keepdims=True))
-        prob_b = prob.astype(BF16)
-        out_blk = dot(vals, prob_b, 0, 0).astype(BF16)
-        o_ref[slot, 0, 0, :, rows] = out_blk
-        o_now_ref[slot, 0, :, rows] = out_blk
-        dpt = dot(vals, do_blk, 1, 0)
-        row_dot = jnp.sum(prob * dpt, axis=0, keepdims=True)
-        dst_b = (prob * (dpt - row_dot)).astype(BF16)
-        dq = dot(keys, dst_b, 0, 0) * scale
+        row_dot = jnp.sum(out * do_blk.astype(F32), axis=0, keepdims=True)
+        for j in range(n_blk):
+            yield True, 2
+            v_slot, v_rows = place[j]
+            dprob = dot(v_ref[v_slot, 0, v_rows, :], do_blk, 1, 0)
+            grad_s[buf, span(j), :] = (score[buf, span(j), :] * ((dprob - row_dot) * inv_sum)).astype(BF16)
+        for j in range(n_blk):
+            yield True, 4
+            dk_part = dot(grad_s[buf, span(j), :], qcat[p], 1, 1)
+            dv_part = dot(prob_b[buf, span(j), :], do_blk, 1, 1)
+            if untouched[j]:
+                dk_acc[span(j), :] = dk_part
+                dv_acc[span(j), :] = dv_part
+                untouched[j] = False
+            else:
+                dk_acc[span(j), :] += dk_part
+                dv_acc[span(j), :] += dv_part
+            pending[j] -= 1
+            if pending[j] == 0:
+                flush(j)
+        yield True, n_blk
+        dq = dot(k_t[:, :n_keys], grad_s[buf, :n_keys, :], 1, 0) * scale
         lead = dq[nope:mid, :]
         tail = dq[mid:, :]
         dq_ref[slot, 0, 0, :nope, rows] = dq[:nope, :].astype(BF16)
         dq_ref[slot, 0, 0, nope:mid, rows] = (lead * cos_p + tail * sin_p).astype(BF16)
         dq_ref[slot, 0, 0, mid:, rows] = (tail * cos_p - lead * sin_p).astype(BF16)
-        dk_part = dot(dst_b, q_blk, 1, 1)
-        dv_part = dot(prob_b, do_blk, 1, 1)
-        if p == 3:
-            dk_acc[...] = dk_part
-            dv_acc[...] = dv_part
-        else:
-            dk_acc[:n_keys, :] += dk_part
-            dv_acc[:n_keys, :] += dv_part
-
-    @pl.when(pl.program_id(0) == 0)
-    def _():
-        dkp_ref[...] = jnp.zeros_like(dkp_ref)
-
-    for p in range(4):
-        slot, rows = where_is(p)
-        src = slice(p * blk, p * blk + blk)
-        dk_ref[slot, 0, rows, :] = (dk_acc[src, :nope] * scale).astype(BF16)
-        dv_ref[slot, 0, rows, :] = dv_acc[src, :].astype(BF16)
-        dkp_ref[slot, rows, :] += dk_acc[src, nope:] * scale
+
+    def stream(blocks, buf):
+        for p in blocks:
+            yield from steps(p, buf)
+
+    streams = [stream((3, 0), 0), stream((2, 1), 1)]
+    heads_of = [next(st) for st in streams]
+    busy = {True: 0, False: 0}
+    while any(nxt is not None for nxt in heads_of):
+        ready = [i for i in range(2) if heads_of[i] is not None]
+        pick = min(ready, key=lambda i: (busy[heads_of[i][0]], i))
+        is_mxu, cost = heads_of[pick]
+        busy[is_mxu] += cost
+        heads_of[pick] = next(streams[pick], None)
 
 
 def attention(batch, rank, q, k, v, kp, do0, do1, cos_t, sin_t, chain):
@@ -158,9 +205,11 @@
             + [pl.BlockSpec(memory_space=pl.ANY)] * n_alias,
             out_specs=[pl.BlockSpec((2, 1, v_dim, seq), lambda h, r: (0, h, 0, 0)),
                        o_spec, dq_spec, k_spec, v_spec, whole(2, seq, rope)],
-            scratch_shapes=[pltpu.VMEM((2 * seq, qk), BF16), pltpu.VMEM((2 * seq, v_dim), BF16),
+            scratch_shapes=[pltpu.VMEM((2 * seq, qk), BF16), pltpu.VMEM((qk, 2 * seq), BF16), pltpu.VMEM((v_dim, 2 * seq), BF16),
                             pltpu.VMEM((4, qk, seq // 2), BF16),
-                            pltpu.VMEM((2 * seq, qk), F32), pltpu.VMEM((2 * seq, v_dim), F32)],
+                            pltpu.VMEM((2 * seq, qk), F32), pltpu.VMEM((2 * seq, v_dim), F32),
+                            pltpu.VMEM((2, 2 * seq, seq // 2), F32), pltpu.VMEM((2, 2 * seq, seq // 2), BF16),
+                            pltpu.VMEM((2, 2 * seq, seq // 2), BF16)],
         ),
         input_output_aliases={9 + i: 1 + i for i in range(n_alias)},
         compiler_params=pltpu.CompilerParams(dimension_semantics=("arbitrary",), vmem_limit_bytes=40 * 2 ** 20),
@@ -208,6 +257,59 @@
     )(rank, mine, other)
 
 
+def head_wgrad_kernel(rank_ref, act_ref, in0_ref, in1_ref, full_ref, mine_ref):
+    n_batch = act_ref.shape[2]
+    total = None
+    for slot, in_ref in ((0, in0_ref), (1, in1_ref)):
+        for b in range(n_batch):
+            act = act_ref[slot, :, b].reshape(-1, act_ref.shape[4])
+            part = dot(act, in_ref[b], 1, 0)
+            total = part if total is None else total + part
+    total = total.reshape(mine_ref.shape)
+    full_ref[...] = total
+    mine_ref[...] = total
+
+
+def head_wgrad(rank, act, in0, in1, tile_h, tile_d):
+    _, heads, n_batch, width, seq = act.shape
+    d_dim = in0.shape[-1]
+    n_h, n_d = heads // tile_h, d_dim // tile_d
+    in_spec = pl.BlockSpec((n_batch, seq, tile_d), lambda d, h, r: (0, 0, d))
+    return pl.pallas_call(
+        head_wgrad_kernel,
+        out_shape=[jax.ShapeDtypeStruct((2 * heads, width, d_dim), F32), jax.ShapeDtypeStruct((heads, width, d_dim), F32)],
+        grid_spec=pltpu.PrefetchScalarGridSpec(
+            num_scalar_prefetch=1, grid=(n_d, n_h),
+            in_specs=[pl.BlockSpec((2, tile_h, n_batch, width, seq), lambda d, h, r: (0, h, 0, 0, 0)), in_spec, in_spec],
+            out_specs=[pl.BlockSpec((tile_h, width, tile_d), lambda d, h, r: (r[0] * n_h + h, 0, d)),
+                       pl.BlockSpec((tile_h, width, tile_d), lambda d, h, r: (h, 0, d))]),
+        compiler_params=pltpu.CompilerParams(dimension_semantics=("arbitrary", "arbitrary"), vmem_limit_bytes=56 * 2 ** 20),
+        cost_estimate=pl.CostEstimate(flops=4 * heads * width * n_batch * seq * d_dim, bytes_accessed=8 * heads * width * d_dim, transcendentals=0),
+        name="head_wgrad",
+    )(rank, act, in0, in1)
+
+
+def fill_kernel(rank_ref, other_ref, whole_ref, out_ref):
+    out_ref[...] = other_ref[...]
+
+
+def fill_other(rank, whole, other, tile_h):
+    heads, width, d_dim = other.shape
+    n_h = heads // tile_h
+    return pl.pallas_call(
+        fill_kernel,
+        out_shape=jax.ShapeDtypeStruct(whole.shape, whole.dtype),
+        grid_spec=pltpu.PrefetchScalarGridSpec(
+            num_scalar_prefetch=1, grid=(n_h,),
+            in_specs=[pl.BlockSpec((tile_h, width, d_dim), lambda h, r: (h, 0, 0)), pl.BlockSpec(memory_space=pl.ANY)],
+            out_specs=pl.BlockSpec((tile_h, width, d_dim), lambda h, r: ((1 - r[0]) * n_h + h, 0, 0))),
+        input_output_aliases={2: 0},
+        compiler_params=pltpu.CompilerParams(dimension_semantics=("arbitrary",), vmem_limit_bytes=48 * 2 ** 20),
+        cost_estimate=pl.CostEstimate(flops=100 * 8 * other.size, bytes_accessed=8 * other.size, transcendentals=0),
+        name="fill_other",
+    )(rank, other, whole)
+
+
 def down_wgrad_kernel(x0_ref, x1_ref, q0_ref, q1_ref, c0_ref, c1_ref, dq_ref, dc_ref):
     x0 = x0_ref[...]
     x1 = x1_ref[...]
@@ -247,7 +349,7 @@
     def with_other(value):
         return jnp.stack([value, swap(value)])
 
-    def per_device(hidden, grad_out, w_dq, g_q, w_dkv, g_kv, w_uq, w_uk, w_uv, w_o):
+    def block(hidden, grad_out, w_dq, g_q, w_dkv, g_kv, w_uq, w_uk, w_uv, w_o):
         cp_rank = lax.axis_index('cp')
         tp_rank = lax.axis_index('tp')
         rank = cp_rank.astype(jnp.int32)[None]
@@ -323,8 +425,16 @@
             dcq_home + swap(dcq_away),
             dckv_home + swap(dckv_away),
             dkp2[0] + swap(dkp2[1])], axis=-1)
-        latent_part, y_parts = lax.optimization_barrier((latent_part, y_parts))
+        latent_part, y_parts, o_all, dq_late = lax.optimization_barrier((latent_part, y_parts, o_all, dq_all))
         latent_grad = lax.psum_scatter(latent_part, 'tp', scatter_dimension=1, tiled=True)
+
+        wo_whole, wo_half = head_wgrad(rank, o_all, grad_out, dy_other, min(4, heads_core), min(1024, hidden.shape[2]))
+        wo_swapped = swap(wo_half)
+        uq_whole, uq_half = head_wgrad(rank, dq_late, c_q2[0], c_q2[1], min(4, heads_core), min(768, q_lora))
+        uq_swapped = swap(uq_half)
+        grad_w_uk = jnp.einsum('sbtc,sbtn->cn', c_kv2, dk_all, preferred_element_type=F32).reshape(kv_lora, heads_core, nope_dim)
+        grad_w_uv = jnp.einsum('sbtc,sbtv->cv', c_kv2, dv_all, preferred_element_type=F32).reshape(kv_lora, heads_core, v_dim)
+        latent_grad, grad_w_uk, grad_w_uv, uq_whole = lax.optimization_barrier((latent_grad, grad_w_uk, grad_w_uv, uq_whole))
 
         def my_tokens(value, axis):
             return lax.dynamic_slice_in_dim(value, tp_rank * tok_tp, tok_tp, axis)
@@ -336,17 +446,17 @@
         grad_kpe_raw = unrope(latent_grad[..., q_lora + kv_lora:], my_tokens(cos_tab, 0), my_tokens(sin_tab, 0))
         draw = jnp.concatenate([grad_cq_raw, grad_ckv_raw, grad_kpe_raw], axis=-1).astype(BF16)
         draw = lax.all_gather(draw, 'tp', axis=1, tiled=True)
-        grad_g_q, grad_g_kv = lax.psum((grad_g_q, grad_g_kv), ('tp', 'cp'))
+        grad_g = jnp.concatenate([grad_g_q, grad_g_kv])
+        for bit in (1, 2):
+            grad_g = grad_g + lax.ppermute(grad_g, 'tp', [(src, src ^ bit) for src in range(tp_size)])
+        grad_g = grad_g + swap(grad_g)
+        grad_g_q, grad_g_kv = grad_g[:q_lora], grad_g[q_lora:]
 
         y_stack, draw = lax.optimization_barrier((jnp.stack(y_parts), draw))
         attn_out = lax.all_gather(y_stack, 'tp', axis=1, tiled=True)
 
-        grad_w_o = jnp.einsum('hbvt,btd->hvd', o_all[0], grad_out, preferred_element_type=F32) + jnp.einsum('hbvt,btd->hvd', o_all[1], dy_other, preferred_element_type=F32)
-        grad_w_uq = jnp.einsum('shbet,sbtq->heq', dq_all, c_q2, preferred_element_type=F32)
-        grad_w_uk = jnp.einsum('sbtc,sbtn->cn', c_kv2, dk_all, preferred_element_type=F32).reshape(kv_lora, heads_core, nope_dim)
-        grad_w_uv = jnp.einsum('sbtc,sbtv->cv', c_kv2, dv_all, preferred_element_type=F32).reshape(kv_lora, heads_core, v_dim)
-        grad_w_o = merge_halves(rank, grad_w_o, swap(grad_w_o), 0, 1)
-        grad_w_uq = jnp.transpose(merge_halves(rank, grad_w_uq, swap(grad_w_uq), 0, 2), (2, 0, 1))
+        grad_w_o = fill_other(rank, wo_whole, wo_swapped, 1)
+        grad_w_uq = jnp.transpose(fill_other(rank, uq_whole, uq_swapped, 2), (2, 0, 1))
         grad_w_uk = merge_halves(rank, grad_w_uk, swap(grad_w_uk), 1, min(kv_lora, 256))
         grad_w_uv = merge_halves(rank, grad_w_uv, swap(grad_w_uv), 1, min(kv_lora, 256))
 
@@ -361,4 +471,4 @@
     head_spec = P(None, 'tp', None)
     out_head_spec = P('tp', None, None)
     all_specs = (seq_spec, seq_spec, full_spec, full_spec, full_spec, full_spec, head_spec, head_spec, head_spec, out_head_spec)
-    return jax.shard_map(per_device, mesh=mesh, in_specs=all_specs, out_specs=all_specs, check_vma=False)
+    return jax.shard_map(block, mesh=mesh, in_specs=all_specs, out_specs=all_specs, check_vma=False)

time: 1240 us -> 1130 us (0.911)
  matrix products: 544 us -> 429 us
  blocking collectives: 23.2 us -> 0 us
  waiting for transfers between devices: 98.1 us -> 121 us
    pallas_call x0 -> x4, Pallas kernels: none -> 178 us  [the longest x2 130 us: head_wgrad(): pl.pallas_call(head_wgrad_kernel, out_shape=[jax.ShapeDtypeStruct((2 * he...]
    dot_general x15 -> x12, matrix products: 391 us -> 272 us  [the longest x3 86.4 us: block(): y_b = jnp.einsum('hvt,hvd->td', o_full, w_o, preferred_element_type=F32)]
    pallas_call x4 -> x2, Pallas kernels: 108 us -> 14.9 us  [merge_halves(): pl.pallas_call(merge_kernel, out_shape=jax.ShapeDtypeStruct(out_shape, mi...]
    pallas_call x3, Pallas kernels: 244 us -> 158 us  [attention(): pl.pallas_call(functools.partial(attn_kernel, qk ** (-0.5), n_alias), out...]
    psum x1 -> x0, blocking collectives: 23.2 us -> none  [per_device(): grad_g_q, grad_g_kv = lax.psum((grad_g_q, grad_g_kv), ('tp', 'cp'))]
    ppermute x17 -> x18, waiting for transfers between devices: 7.67 us -> 27.9 us  [swap(): return lax.ppermute(value, 'cp', swap_pairs)]
    reduce_scatter x4, waiting for transfers between devices: 38 us -> 23.5 us  [the longest x3 23.5 us: block(): lax.psum_scatter(y_b, 'tp', scatter_dimension=0, tiled=True).astype(BF16)]
    all_gather x2, waiting for transfers between devices: 52.4 us -> 64.8 us  [the longest x1 64.8 us: block(): draw = lax.all_gather(draw, 'tp', axis=1, tiled=True)]
  transfers between devices with their start and end apart: 23 -> 26, of which waited for: 4 -> 9; matrix products, arithmetic and copies ran while one was open for 44% -> 38% of each run, Pallas kernels for 28% -> 34%
where the time goes in v2:
time: 1130 us; the launch traced here: 1120 us
  matrix products  429 us (38%)
  Pallas kernels  429 us (38%)
  waiting for transfers between devices  121 us (11%)
  local copies, waits for them, and re-layouts  72.4 us (6%)
  other arithmetic  45 us (4%)
  between operations  15.3 us (1%)
    pallas_call x3, Pallas kernels, attention(): pl.pallas_call(functools.partial(attn_kernel, qk ** (-0.5), n_alias), out...  158 us
    pallas_call x2, Pallas kernels, head_wgrad(): pl.pallas_call(head_wgrad_kernel, out_shape=[jax.ShapeDtypeStruct((2 * he...  130 us
    dot_general x3, matrix products, block(): y_b = jnp.einsum('hvt,hvd->td', o_full, w_o, preferred_element_type=F32)  86.4 us
    dot_general x2, matrix products, head_grads(): jnp.einsum('hvd,btd->hbvt', wo_mine, dy, preferred_element_type=F32)  82.8 us
    pallas_call x1, Pallas kernels, down_wgrad(): pl.pallas_call(down_wgrad_kernel, out_shape=[jax.ShapeDtypeStruct((width,...  77.8 us
    all_gather x1, waiting for transfers between devices, block(): draw = lax.all_gather(draw, 'tp', axis=1, tiled=True)  64.8 us
    pallas_call x2, Pallas kernels, fill_other(): pl.pallas_call(fill_kernel, out_shape=jax.ShapeDtypeStruct(whole.shape, w...  48.3 us
    dot_general x2, matrix products, latent_grads(): jnp.einsum('hbet,heq->btq', dq_all[slot], uq_mine, preferred_element_type...  44.9 us
  transfers between devices with their start and end apart: 26, of which 9 were waited for; matrix products, arithmetic and copies ran while one was open for 38% of the time, Pallas kernels for 34%

profile of v2, /device:TPU:0, one launch (start us, length us, event | category | flops | bytes accessed | tf_op | source)
XLA Modules:
  0.0 1118.8 jit_solution(11778434558837074687)
XLA Ops:
  7.3 17.1 %fusion.99 = bf16[3,512,576]{2,1,0:T(8,128)(2,1)S(1)} fusion(bf16[3,512,5120]{2,1,0:T(8,128)(2,1)} %param.10, bf16[5120,576]{0,1:T(8,128)(2,1)} %param.14), kind=kOutput, calls=%fused_computation.106 | convolution fusion | flops 9060581376 | bytes 23396352 | tf_op jit(solution)/shard_map/btd,dc->btc/dot_general | solution.py:378
  29.3 32.0 %fusion.16 = (f32[3,512]{1,0:T(4,128)S(1)}, bf16[3,512,1536]{2,1,0:T(8,128)(2,1)S(1)}) fusion(bf16[3,512,5120]{2,1,0:T(8,128)(2,1)} %param.10, bf16[5120,1536]{1,0:T(8,128)(2,1)} %param.12), kind=kOutput, calls=%fused_computation.21 | convolution fusion | flops 24168626176 | bytes 36182016 | tf_op jit(solution)/shard_map/btd,dq->btq/dot_general | solution.py:377
  65.5 41.5 %convert_bitcast_fusion.2.do0_ref = bf16[16,3,128,512]{3,2,1,0:T(8,128)(2,1)} fusion(bf16[3,512,5120]{2,1,0:T(8,128)(2,1)} %in0_ref.1, bf16[32,128,5120]{2,1,0:T(8,128)(2,1)} %param.19, s32[]{:T(128)S(6)} %select_n.59), kind=kOutput, calls=%fused_computation.58 | convolution fusion | flops 32215400448 | bytes 42991620 | tf_op jit(solution)/shard_map/hvd,btd->hbvt/dot_general | solution.py:391
  126.3 11.2 %convolution_convert_fusion.v_ref = bf16[2,3,512,2048]{3,2,1,0:T(8,128)(2,1)} fusion(bf16[512,2048,1,1]{1,0,2,3:T(8,128)(2,1)S(1)} %copy-done.16, bf16[1,3,512,512]{3,2,1,0:T(8,128)(2,1)} %bitcast.11, bf16[1,3,512,512]{3,2,1,0:T(8,128)(2,1)S(1)} %fusion.141), kind=kOutput, calls=%fused_computation.43 | convolution fusion | flops 6450315264 | bytes 17825792 | tf_op jit(solution)/shard_map/sbtc,cv->sbtv/dot_general | solution.py:397
  137.5 11.3 %convolution_convert_fusion.1.k_ref = bf16[2,3,512,2048]{3,2,1,0:T(8,128)(2,1)} fusion(bf16[512,2048,1,1]{1,0,2,3:T(8,128)(2,1)S(1)} %copy-done.17, bf16[1,3,512,512]{3,2,1,0:T(8,128)(2,1)} %bitcast.11, bf16[1,3,512,512]{3,2,1,0:T(8,128)(2,1)S(1)} %fusion.141), kind=kOutput, calls=%fused_computation.44 | convolution fusion | flops 6450315264 | bytes 17825792 | tf_op jit(solution)/shard_map/sbtc,cn->sbtn/dot_general | solution.py:396
  148.8 35.0 %convert_bitcast_fusion.q_ref = bf16[16,2,3,192,512]{4,3,2,1,0:T(8,128)(2,1)} fusion(bf16[1,3,512,1536]{3,2,1,0:T(8,128)(2,1)} %bitcast.3, bf16[1,3,512,1536]{3,2,1,0:T(8,128)(2,1)S(1)} %fusion.142, bf16[1536,32,192]{0,2,1:T(8,128)(2,1)} %param.16, s32[]{:T(128)S(6)} %select_n.59), kind=kOutput, calls=%fused_computation.5 | convolution fusion | flops 29019340800 | bytes 37748740 | tf_op jit(solution)/shard_map/heq,sbtq->hsbet/dot_general | solution.py:395
  183.8 41.3 %convert_bitcast_fusion.1.do1_ref = bf16[16,3,128,512]{3,2,1,0:T(8,128)(2,1)} fusion(bf16[3,512,5120]{2,1,0:T(8,128)(2,1)} %collective-permute-done.3.in1_ref, bf16[32,128,5120]{2,1,0:T(8,128)(2,1)} %param.19, s32[]{:T(128)S(6)} %select_n.59), kind=kOutput, calls=%fused_computation.57 | convolution fusion | flops 32215400448 | bytes 42991620 | tf_op jit(solution)/shard_map/hvd,btd->hbvt/dot_general | solution.py:391
  227.9 52.8 %attn_fwd_bwd.3 = (bf16[2,16,128,512]{3,2,1,0:T(8,128)(2,1)S(1)}, bf16[2,16,3,128,512]{4,3,2,1,0:T(8,128)(2,1)}, bf16[2,16,3,192,512]{4,3,2,1,0:T(8,128)(2,1)}, ...) custom-call(s32[1]{0:T(128)} %bitcast.rank_ref, ...), custom_call_target="tpu_custom_call" | custom-call | flops 16777216000 | bytes 33554432 | tf_op jit(solution)/shard_map/attn_fwd_bwd/pallas_call | solution.py:197
  291.3 28.8 %convolution_bitcast_fusion.2 = f32[512,5120]{1,0:T(8,128)} fusion(bf16[32,128,5120]{2,1,0:T(8,128)(2,1)} %param.19, bf16[16,128,512]{2,1,0:T(8,128)(2,1)S(1)} %get-tuple-element.129, bf16[16,128,512]{2,1,0:T(8,128)(2,1)S(1)} %get-tuple-element.128), kind=kOutput, calls=%fused_computation.39 | convolution fusion | flops 21476933632 | bytes 56623104 | tf_op jit(solution)/shard_map/hvt,hvd->td/dot_general | solution.py:411
  323.0 52.6 %attn_fwd_bwd.4 = (bf16[2,16,128,512]{3,2,1,0:T(8,128)(2,1)S(1)}, bf16[2,16,3,128,512]{4,3,2,1,0:T(8,128)(2,1)}, bf16[2,16,3,192,512]{4,3,2,1,0:T(8,128)(2,1)}, ...) custom-call(s32[1]{0:T(128)} %bitcast.rank_ref, ...), custom_call_target="tpu_custom_call", output_to_operand_aliasing={{1}: (9, {}), {2}: (10, {}), {3}: (11, {}), {4}: (12, {})} | custom-call | flops 16777216000 | bytes 33554432 | tf_op jit(solution)/shard_map/attn_fwd_bwd/pallas_call | solution.py:197
  380.2 28.7 %convolution_bitcast_fusion.1 = f32[512,5120]{1,0:T(8,128)} fusion(bf16[32,128,5120]{2,1,0:T(8,128)(2,1)} %param.19, bf16[16,128,512]{2,1,0:T(8,128)(2,1)S(1)} %get-tuple-element.127, bf16[16,128,512]{2,1,0:T(8,128)(2,1)S(1)} %get-tuple-element.126), kind=kOutput, calls=%fused_computation.38 | convolution fusion | flops 21476933632 | bytes 56623104 | tf_op jit(solution)/shard_map/hvt,hvd->td/dot_general | solution.py:411
  411.9 52.6 %attn_fwd_bwd.5 = (bf16[2,16,128,512]{3,2,1,0:T(8,128)(2,1)S(1)}, bf16[2,16,3,128,512]{4,3,2,1,0:T(8,128)(2,1)}, bf16[2,16,3,192,512]{4,3,2,1,0:T(8,128)(2,1)}, ...) custom-call(s32[1]{0:T(128)} %bitcast.rank_ref, ...), custom_call_target="tpu_custom_call", output_to_operand_aliasing={{1}: (9, {}), {2}: (10, {}), {3}: (11, {}), {4}: (12, {})} | custom-call | flops 16777216000 | bytes 33554432 | tf_op jit(solution)/shard_map/attn_fwd_bwd/pallas_call | solution.py:197
  469.2 28.9 %convolution_bitcast_fusion = f32[512,5120]{1,0:T(8,128)} fusion(bf16[32,128,5120]{2,1,0:T(8,128)(2,1)} %param.19, bf16[16,128,512]{2,1,0:T(8,128)(2,1)S(1)} %get-tuple-element.125, bf16[16,128,512]{2,1,0:T(8,128)(2,1)S(1)} %get-tuple-element.124), kind=kOutput, calls=%fused_computation.37 | convolution fusion | flops 21476933632 | bytes 56623104 | tf_op jit(solution)/shard_map/hvt,hvd->td/dot_general | solution.py:411
  498.1 22.4 %fusion.52 = f32[3,512,1536]{2,1,0:T(8,128)} fusion(bf16[1536,32,192]{0,2,1:T(8,128)(2,1)} %param.16, s32[]{:T(128)S(6)} %select_n.59, bf16[2,16,3,192,512]{4,3,2,1,0:T(8,128)(2,1)} %get-tuple-element.103.act_ref), kind=kOutput, calls=%fused_computation.62 | convolution fusion | flops 14495514624 | bytes 28311556 | tf_op jit(solution)/shard_map/hbet,heq->btq/dot_general | solution.py:417
  535.8 8.4 fusion.104
  559.5 7.8 add_add_fusion.1
  567.4 22.4 %bitcast_add_fusion = f32[3,512,1536]{2,1,0:T(8,128)S(1)} fusion(f32[3,512,1536]{2,1,0:T(8,128)} %collective-permute-done.7, bf16[1536,32,192]{0,2,1:T(8,128)(2,1)} %param.16, s32[]{:T(128)S(6)} %select_n.59, bf16[2,16,3,192,512]{4,3,2,1,0:T(8,128)(2,1)} %get-tuple-element.103.act_ref), kind=kOutput, calls=%fused_computation.33 | convolution fusion | flops 14497873920 | bytes 37748740 | tf_op jit(solution)/shard_map/hbet,heq->btq/dot_general | solution.py:417
  600.1 23.5 %reduce-scatter.9.cloned.1.call-done = f32[128,5120]{1,0:T(8,128)} async-done(((f32[512,5120]{1,0:T(8,128)}), f32[128,5120]{1,0:T(8,128)}) %reduce-scatter.9.cloned.1.call-update) | async-done | bytes 2621456 | tf_op jit(solution)/shard_map/reduce_scatter | solution.py:413
  626.6 90.0 %head_wgrad.3 = (f32[32,128,5120]{2,1,0:T(8,128)}, f32[16,128,5120]{2,1,0:T(8,128)}) custom-call(s32[1]{0:T(128)} %bitcast.rank_ref, bf16[2,16,3,128,512]{4,3,2,1,0:T(8,128)(2,1)} %get-tuple-element.117.act_ref, bf16[3,512,5120]{2,1,0:T(8,128)(2,1)} %in0_ref.1, bf16[3,512,5120]{2,1,0:T(8,128)(2,1)} %collective-permute-done.3.in1_ref), custom_call_target="tpu_custom_call" | custom-call | flops 64424509440 | bytes 83886080 | tf_op jit(solution)/shard_map/head_wgrad/pallas_call | solution.py:278
  720.1 11.0 fusion.87
  734.1 40.1 %head_wgrad.2 = (f32[32,192,1536]{2,1,0:T(8,128)}, f32[16,192,1536]{2,1,0:T(8,128)}) custom-call(s32[1]{0:T(128)} %bitcast.rank_ref, bf16[2,16,3,192,512]{4,3,2,1,0:T(8,128)(2,1)} %get-tuple-element.103.act_ref, bf16[3,512,1536]{2,1,0:T(8,128)(2,1)} %fusion.18.in0_ref, bf16[3,512,1536]{2,1,0:T(8,128)(2,1)} %collective-permute-done.in1_ref), custom_call_target="tpu_custom_call" | custom-call | flops 28991029248 | bytes 37748736 | tf_op jit(solution)/shard_map/head_wgrad/pallas_call | solution.py:278
  774.4 10.4 fusion.92
  803.8 64.8 %all-gather.3.cloned.1.call-done = bf16[3,512,2112]{2,1,0:T(8,128)(2,1)} async-done(((bf16[3,128,2112]{2,1,0:T(8,128)(2,1)}), bf16[3,512,2112]{2,1,0:T(8,128)(2,1)}) %all-gather.3.cloned.1.call-update) | async-done | bytes 6488080 | tf_op jit(solution)/shard_map/all_gather | solution.py:448
  876.6 16.5 %fill_other.2 = f32[32,192,1536]{2,1,0:T(8,128)} custom-call(s32[1]{0:T(128)} %bitcast.rank_ref, f32[16,192,1536]{2,1,0:T(8,128)} %collective-permute-done.16.other_ref, f32[32,192,1536]{2,1,0:T(8,128)} %get-tuple-element.114.whole_ref), custom_call_target="tpu_custom_call", output_to_operand_aliasing={{}: (2, {})} | custom-call | flops 3774873600 | bytes 37748736 | tf_op jit(solution)/shard_map/fill_other/pallas_call | solution.py:299
  893.0 11.6 %collective-permute-done.15 = f32[2048]{0:T(1024)S(1)} collective-permute-done((f32[2048]{0:T(1024)S(1)}, f32[2048]{0:T(1024)S(1)}, u32[]{:S(2)}, u32[]{:S(2)}) %collective-permute-start.15) | collective-permute-done | bytes 8224 | tf_op jit(solution)/shard_map/ppermute | solution.py:347
  905.3 7.8 merge_halves.3
  913.1 7.1 merge_halves.2
  924.6 34.0 %fusion.8 = f32[3,512,5120]{2,1,0:T(8,128)} fusion(bf16[3,512,1536]{2,1,0:T(8,128)(2,1)} %slice.110, bf16[5120,1536]{1,0:T(8,128)(2,1)} %param.12), kind=kOutput, calls=%fused_computation.10 | convolution fusion | flops 24159191040 | bytes 51904512 | tf_op jit(solution)/shard_map/btq,dq->btd/dot_general | solution.py:465
  960.8 23.9 %add_convert_fusion = bf16[3,512,5120]{2,1,0:T(8,128)(2,1)} fusion(f32[3,512,5120]{2,1,0:T(8,128)} %fusion.8, bf16[3,512,576]{2,1,0:T(8,128)(2,1)S(1)} %slice.111, bf16[5120,576]{0,1:T(8,128)(2,1)} %param.14), kind=kOutput, calls=%fused_computation | convolution fusion | flops 9075425280 | bytes 54853632 | tf_op jit(solution)/shard_map/btc,dc->btd/dot_general | solution.py:465
  988.6 77.8 %down_wgrad.1 = (f32[5120,1536]{1,0:T(8,128)}, f32[576,5120]{1,0:T(8,128)}) custom-call(bf16[1536,5120]{1,0:T(8,128)(2,1)} %bitcast.195, bf16[1536,5120]{1,0:T(8,128)(2,1)} %bitcast.58.x1_ref, bf16[1536,1536]{1,0:T(8,128)(2,1)} %bitcast.59.q0_ref, bf16[1536,1536]{1,0:T(8,128)(2,1)} %bitcast.60.q1_ref, bf16[1536,576]{1,0:T(8,128)(2,1)} %bitcast.184, ...), custom_call_target="tpu_custom_call" | custom-call | flops 66437775360 | bytes 74711040 | tf_op jit(solution)/shard_map/down_wgrad/pallas_call | solution.py:328
  1066.5 31.9 %fill_other.3 = f32[32,128,5120]{2,1,0:T(8,128)} custom-call(s32[1]{0:T(128)} %bitcast.rank_ref, f32[16,128,5120]{2,1,0:T(8,128)} %collective-permute-done.19.other_ref, f32[32,128,5120]{2,1,0:T(8,128)} %get-tuple-element.119.whole_ref), custom_call_target="tpu_custom_call", output_to_operand_aliasing={{}: (2, {})} | custom-call | flops 8388608000 | bytes 83886080 | tf_op jit(solution)/shard_map/fill_other/pallas_call | solution.py:299
  1098.3 13.2 %copy.112 = bf16[3,512,5120]{2,1,0:T(8,128)(2,1)} copy(bf16[3,512,5120]{2,1,0:T(8,128)(2,1)} %all-gather.5.cloned.1.call-done) | data formatting | bytes 31457280
  (203 shorter events, 145.2 us)
Async XLA Ops:
  7.2 588.0 %reduce-scatter.5.cloned.1.call-start = ((), (), s32[]{:S(2)}) async-start(), calls=%async_computation.4 | async-start | bytes 13107200 | tf_op jit(solution)/shard_map/reduce_scatter | solution.py:413
  24.3 95.8 %copy-start.7 = (bf16[3,512,576]{2,1,0:T(8,128)(2,1)}, bf16[3,512,576]{2,1,0:T(8,128)(2,1)S(1)}, u32[]{:S(2)}) copy-start(bf16[3,512,576]{2,1,0:T(8,128)(2,1)S(1)} %fusion.99) | copy-start | bytes 5308420
  26.4 99.5 %collective-permute-start.2 = (bf16[3,512,64]{2,1,0:T(8,128)(2,1)S(1)}, bf16[3,512,64]{2,1,0:T(8,128)(2,1)S(1)}, u32[]{:S(2)}, u32[]{:S(2)}) collective-permute-start(bf16[3,512,64]{2,1,0:T(8,128)(2,1)S(1)} %pad_maximum_fusion.5), channel_id=1, source_target_pairs={{0,1},{1,0},{2,3},{3,2},{4,5},{5,4},{6,7},{7,6}} | collective-permute-start | bytes 589832 | tf_op jit(solution)/shard_map/ppermute | solution.py:347
  29.3 97.0 %collective-permute-start.1 = (bf16[3,512,512]{2,1,0:T(8,128)(2,1)}, bf16[3,512,512]{2,1,0:T(8,128)(2,1)}, u32[]{:S(2)}, u32[]{:S(2)}) collective-permute-start(bf16[3,512,512]{2,1,0:T(8,128)(2,1)} %fusion.79), channel_id=1, source_target_pairs={{0,1},{1,0},{2,3},{3,2},{4,5},{5,4},{6,7},{7,6}} | collective-permute-start | bytes 4718600 | tf_op jit(solution)/shard_map/ppermute | solution.py:347
  61.3 60.0 %copy-start.24 = (f32[1536]{0:T(1024)}, f32[1536]{0:T(1024)S(1)}, u32[]{:S(2)}) copy-start(f32[1536]{0:T(1024)S(1)} %convert_element_type.102) | copy-start | bytes 18436
  65.0 83.9 %collective-permute-start = (bf16[3,512,1536]{2,1,0:T(8,128)(2,1)}, bf16[3,512,1536]{2,1,0:T(8,128)(2,1)}, u32[]{:S(2)}, u32[]{:S(2)}) collective-permute-start(bf16[3,512,1536]{2,1,0:T(8,128)(2,1)} %fusion.18.in0_ref), channel_id=1, source_target_pairs={{0,1},{1,0},{2,3},{3,2},{4,5},{5,4},{6,7},{7,6}} | collective-permute-start | bytes 14155784 | tf_op jit(solution)/shard_map/ppermute | solution.py:347
  65.4 118.4 %collective-permute-start.3 = (bf16[3,512,5120]{2,1,0:T(8,128)(2,1)}, bf16[3,512,5120]{2,1,0:T(8,128)(2,1)}, u32[]{:S(2)}, u32[]{:S(2)}) collective-permute-start(bf16[3,512,5120]{2,1,0:T(8,128)(2,1)} %in0_ref.1), channel_id=1, source_target_pairs={{0,1},{1,0},{2,3},{3,2},{4,5},{5,4},{6,7},{7,6}} | collective-permute-start | bytes 47185928 | tf_op jit(solution)/shard_map/ppermute | solution.py:347
  284.2 4.6 collective-permute-start.4
  320.1 277.0 %reduce-scatter.7.cloned.1.call-start = ((), (), s32[]{:S(2)}) async-start(), calls=%async_computation.5 | async-start | bytes 13107200 | tf_op jit(solution)/shard_map/reduce_scatter | solution.py:413
  375.7 4.2 collective-permute-start.5
  408.9 214.6 %reduce-scatter.9.cloned.1.call-start = ((), (), s32[]{:S(2)}) async-start(), calls=%async_computation.6 | async-start | bytes 13107200 | tf_op jit(solution)/shard_map/reduce_scatter | solution.py:413
  464.7 4.2 collective-permute-start.6
  498.1 289.6 %reduce-scatter.11.cloned.1.call-start = ((), (), s32[]{:S(2)}) async-start(), calls=%async_computation.7 | async-start | bytes 16711680 | tf_op jit(solution)/shard_map/reduce_scatter | solution.py:429
  520.6 46.8 %collective-permute-start.7 = (f32[3,512,1536]{2,1,0:T(8,128)}, f32[3,512,1536]{2,1,0:T(8,128)}, u32[]{:S(2)}, u32[]{:S(2)}) collective-permute-start(f32[3,512,1536]{2,1,0:T(8,128)} %fusion.52), channel_id=1, source_target_pairs={{0,1},{1,0},{2,3},{3,2},{4,5},{5,4},{6,7},{7,6}} | collective-permute-start | bytes 28311560 | tf_op jit(solution)/shard_map/ppermute | solution.py:347
  544.2 15.4 %collective-permute-start.8 = (f32[3,512,512]{2,1,0:T(8,128)}, f32[3,512,512]{2,1,0:T(8,128)}, u32[]{:S(2)}, u32[]{:S(2)}) collective-permute-start(f32[3,512,512]{2,1,0:T(8,128)} %fusion.104), channel_id=1, source_target_pairs={{0,1},{1,0},{2,3},{3,2},{4,5},{5,4},{6,7},{7,6}} | collective-permute-start | bytes 9437192 | tf_op jit(solution)/shard_map/ppermute | solution.py:347
  545.8 4.9 collective-permute-start.9
  626.6 90.0 %copy-start.8 = (bf16[3,512,576]{2,1,0:T(8,128)(2,1)S(1)}, bf16[3,512,576]{2,1,0:T(8,128)(2,1)}, u32[]{:S(2)}) copy-start(bf16[3,512,576]{2,1,0:T(8,128)(2,1)} %copy-done.7) | copy-start | bytes 5308420
  626.6 242.0 %all-gather.3.cloned.1.call-start = ((), (), s32[]{:S(2)}) async-start(), calls=%async_computation.8 | async-start | bytes 8355840 | tf_op jit(solution)/shard_map/all_gather | solution.py:448
  716.6 349.8 %collective-permute-start.19 = (f32[16,128,5120]{2,1,0:T(8,128)}, f32[16,128,5120]{2,1,0:T(8,128)}, u32[]{:S(2)}, u32[]{:S(2)}) collective-permute-start(f32[16,128,5120]{2,1,0:T(8,128)} %get-tuple-element.118), channel_id=1, source_target_pairs={{0,1},{1,0},{2,3},{3,2},{4,5},{5,4},{6,7},{7,6}} | collective-permute-start | bytes 125829128 | tf_op jit(solution)/shard_map/ppermute | solution.py:347
  720.1 67.6 %copy-start.31 = (f32[3,128]{1,0:T(4,128)}, f32[3,128]{1,0:T(4,128)S(1)}, u32[]{:S(2)}) copy-start(f32[3,128]{1,0:T(4,128)S(1)} %fusion.124) | copy-start | bytes 4612
  720.1 69.8 %copy-start.30 = (f32[3,128]{1,0:T(4,128)}, f32[3,128]{1,0:T(4,128)S(1)}, u32[]{:S(2)}) copy-start(f32[3,128]{1,0:T(4,128)S(1)} %fusion.123) | copy-start | bytes 4612
  774.2 101.8 %collective-permute-start.16 = (f32[16,192,1536]{2,1,0:T(8,128)}, f32[16,192,1536]{2,1,0:T(8,128)}, u32[]{:S(2)}, u32[]{:S(2)}) collective-permute-start(f32[16,192,1536]{2,1,0:T(8,128)} %get-tuple-element.113), channel_id=1, source_target_pairs={{0,1},{1,0},{2,3},{3,2},{4,5},{5,4},{6,7},{7,6}} | collective-permute-start | bytes 56623112 | tf_op jit(solution)/shard_map/ppermute | solution.py:347
  800.5 297.8 %all-gather.5.cloned.1.call-start = ((), (), s32[]{:S(2)}) async-start(), calls=%async_computation.9 | async-start | bytes 19660800 | tf_op jit(solution)/shard_map/all_gather | solution.py:456
  800.6 68.1 %copy-start.33 = (f32[512]{0:T(512)S(1)}, f32[512]{0:T(512)}, u32[]{:S(2)}) copy-start(f32[512]{0:T(512)} %get-tuple-element.122) | copy-start | bytes 6148
  868.6 120.0 %collective-permute-start.10 = (bf16[3,512,5120]{2,1,0:T(8,128)(2,1)}, bf16[3,512,5120]{2,1,0:T(8,128)(2,1)}, u32[]{:S(2)}, u32[]{:S(2)}) collective-permute-start(bf16[3,512,5120]{2,1,0:T(8,128)(2,1)} %param.10), channel_id=1, source_target_pairs={{0,1},{1,0},{2,3},{3,2},{4,5},{5,4},{6,7},{7,6}} | collective-permute-start | bytes 47185928 | tf_op jit(solution)/shard_map/ppermute | solution.py:347
  868.7 3.7 collective-permute-start.13
  870.2 35.1 %collective-permute-start.18 = (f32[512,16,128]{2,1,0:T(8,128)}, f32[512,16,128]{2,1,0:T(8,128)}, u32[]{:S(2)}, u32[]{:S(2)}) collective-permute-start(f32[512,16,128]{2,1,0:T(8,128)} %bitcast.178), channel_id=1, source_target_pairs={{0,1},{1,0},{2,3},{3,2},{4,5},{5,4},{6,7},{7,6}} | collective-permute-start | bytes 12582920 | tf_op jit(solution)/shard_map/ppermute | solution.py:347
  872.4 3.7 collective-permute-start.14
  876.0 37.1 %collective-permute-start.17 = (f32[512,16,128]{2,1,0:T(8,128)}, f32[512,16,128]{2,1,0:T(8,128)}, u32[]{:S(2)}, u32[]{:S(2)}) collective-permute-start(f32[512,16,128]{2,1,0:T(8,128)} %bitcast.176), channel_id=1, source_target_pairs={{0,1},{1,0},{2,3},{3,2},{4,5},{5,4},{6,7},{7,6}} | collective-permute-start | bytes 12582920 | tf_op jit(solution)/shard_map/ppermute | solution.py:347
  876.0 28.6 %collective-permute-start.15 = (f32[2048]{0:T(1024)S(1)}, f32[2048]{0:T(1024)S(1)}, u32[]{:S(2)}, u32[]{:S(2)}) collective-permute-start(f32[2048]{0:T(1024)S(1)} %add.123), channel_id=1, source_target_pairs={{0,1},{1,0},{2,3},{3,2},{4,5},{5,4},{6,7},{7,6}} | collective-permute-start | bytes 24584 | tf_op jit(solution)/shard_map/ppermute | solution.py:347
  924.5 64.1 %collective-permute-start.11 = (bf16[3,512,1536]{2,1,0:T(8,128)(2,1)}, bf16[3,512,1536]{2,1,0:T(8,128)(2,1)}, u32[]{:S(2)}, u32[]{:S(2)}) collective-permute-start(bf16[3,512,1536]{2,1,0:T(8,128)(2,1)} %slice.110), channel_id=1, source_target_pairs={{0,1},{1,0},{2,3},{3,2},{4,5},{5,4},{6,7},{7,6}} | collective-permute-start | bytes 14155784 | tf_op jit(solution)/shard_map/ppermute | solution.py:347
  960.8 23.9 %collective-permute-start.12 = (bf16[3,512,576]{1,2,0:T(8,128)(2,1)}, bf16[3,512,576]{1,2,0:T(8,128)(2,1)}, u32[]{:S(2)}, u32[]{:S(2)}) collective-permute-start(bf16[3,512,576]{1,2,0:T(8,128)(2,1)} %copy.60), channel_id=1, source_target_pairs={{0,1},{1,0},{2,3},{3,2},{4,5},{5,4},{6,7},{7,6}} | collective-permute-start | bytes 5308424 | tf_op jit(solution)/shard_map/ppermute | solution.py:347
  (35 other events, 304.1 us)
Sparse Core Ops, SparseCore 0:
  320.3 100.2 reduce-scatter.4
  424.1 97.8 reduce-scatter.6
  525.7 97.8 reduce-scatter.8
  627.1 121.4 reduce-scatter.10
  800.6 67.9 all-gather.2
  870.2 142.9 all-gather.4

commit v3 on v2

--- a/solution.py
+++ b/solution.py
@@ -259,10 +259,12 @@
 
 def head_wgrad_kernel(rank_ref, act_ref, in0_ref, in1_ref, full_ref, mine_ref):
     n_batch = act_ref.shape[2]
+    tile_h = mine_ref.shape[0]
+    head0 = pl.program_id(1) * tile_h
     total = None
     for slot, in_ref in ((0, in0_ref), (1, in1_ref)):
         for b in range(n_batch):
-            act = act_ref[slot, :, b].reshape(-1, act_ref.shape[4])
+            act = act_ref[slot, pl.ds(head0, tile_h), b].reshape(-1, act_ref.shape[4])
             part = dot(act, in_ref[b], 1, 0)
             total = part if total is None else total + part
     total = total.reshape(mine_ref.shape)
@@ -280,7 +282,7 @@
         out_shape=[jax.ShapeDtypeStruct((2 * heads, width, d_dim), F32), jax.ShapeDtypeStruct((heads, width, d_dim), F32)],
         grid_spec=pltpu.PrefetchScalarGridSpec(
             num_scalar_prefetch=1, grid=(n_d, n_h),
-            in_specs=[pl.BlockSpec((2, tile_h, n_batch, width, seq), lambda d, h, r: (0, h, 0, 0, 0)), in_spec, in_spec],
+            in_specs=[pl.BlockSpec(act.shape, lambda d, h, r: (0, 0, 0, 0, 0), pipeline_mode=pl.Buffered(1)), in_spec, in_spec],
             out_specs=[pl.BlockSpec((tile_h, width, tile_d), lambda d, h, r: (r[0] * n_h + h, 0, d)),
                        pl.BlockSpec((tile_h, width, tile_d), lambda d, h, r: (h, 0, d))]),
         compiler_params=pltpu.CompilerParams(dimension_semantics=("arbitrary", "arbitrary"), vmem_limit_bytes=56 * 2 ** 20),
@@ -410,7 +412,8 @@
             o_full = jnp.concatenate([jnp.where(cp_rank == 0, o_now[0], o_recv), jnp.where(cp_rank == 0, o_recv, o_now[0])], axis=0)
             y_b = jnp.einsum('hvt,hvd->td', o_full, w_o, preferred_element_type=F32)
             chain, y_b = lax.optimization_barrier((chain, y_b))
-            y_parts.append(lax.psum_scatter(y_b, 'tp', scatter_dimension=0, tiled=True).astype(BF16))
+            y_b = lax.psum_scatter(y_b, 'tp', scatter_dimension=0, tiled=True)
+            y_parts.append(y_b.astype(BF16))
         o_all, dq_all, dk_all, dv_all = chain
 
         def latent_grads(slot):
@@ -425,7 +428,7 @@
             dcq_home + swap(dcq_away),
             dckv_home + swap(dckv_away),
             dkp2[0] + swap(dkp2[1])], axis=-1)
-        latent_part, y_parts, o_all, dq_late = lax.optimization_barrier((latent_part, y_parts, o_all, dq_all))
+        latent_part, o_all, dq_late = lax.optimization_barrier((latent_part, o_all, dq_all))
         latent_grad = lax.psum_scatter(latent_part, 'tp', scatter_dimension=1, tiled=True)
 
         wo_whole, wo_half = head_wgrad(rank, o_all, grad_out, dy_other, min(4, heads_core), min(1024, hidden.shape[2]))
@@ -456,9 +459,11 @@
         attn_out = lax.all_gather(y_stack, 'tp', axis=1, tiled=True)
 
         grad_w_o = fill_other(rank, wo_whole, wo_swapped, 1)
-        grad_w_uq = jnp.transpose(fill_other(rank, uq_whole, uq_swapped, 2), (2, 0, 1))
-        grad_w_uk = merge_halves(rank, grad_w_uk, swap(grad_w_uk), 1, min(kv_lora, 256))
-        grad_w_uv = merge_halves(rank, grad_w_uv, swap(grad_w_uv), 1, min(kv_lora, 256))
+        grad_w_uq = fill_other(rank, uq_whole, uq_swapped, 2)
+        grad_w_uq = jnp.transpose(grad_w_uq, (2, 0, 1))
+        uk_swapped, uv_swapped = swap(grad_w_uk), swap(grad_w_uv)
+        grad_w_uk = merge_halves(rank, grad_w_uk, uk_swapped, 1, min(kv_lora, 256))
+        grad_w_uv = merge_halves(rank, grad_w_uv, uv_swapped, 1, min(kv_lora, 256))
 
         dcq_raw, dkv_raw = lax.optimization_barrier((draw[..., :q_lora], draw[..., q_lora:]))
         dcq_other, dkv_other = swap(dcq_raw), swap(dkv_raw)

time: 1130 us -> 1350 us (1.19)
  waiting for transfers between devices: 121 us -> 355 us
    reduce_scatter x3, waiting for transfers between devices: 23.5 us -> 255 us  [block(): y_b = lax.psum_scatter(y_b, 'tp', scatter_dimension=0, tiled=True)]
    unnamed x85 -> x73, local copies, waits for them, and re-layouts: 31.2 us -> 31.1 us
  transfers between devices with their start and end apart: 26 -> 26, of which waited for: 9 -> 11; matrix products, arithmetic and copies ran while one was open for 38% -> 23% of each run, Pallas kernels for 34% -> 20%
where the time goes in v3:
time: 1350 us; the launch traced here: 1340 us
  matrix products  426 us (32%)
  Pallas kernels  425 us (31%)
  waiting for transfers between devices  355 us (26%)
  local copies, waits for them, and re-layouts  70.6 us (5%)
  other arithmetic  39.4 us (3%)
  between operations  15.2 us (1%)
    reduce_scatter x3, waiting for transfers between devices, block(): y_b = lax.psum_scatter(y_b, 'tp', scatter_dimension=0, tiled=True)  255 us
    pallas_call x3, Pallas kernels, attention(): pl.pallas_call(functools.partial(attn_kernel, qk ** (-0.5), n_alias), out...  158 us
    pallas_call x2, Pallas kernels, head_wgrad(): pl.pallas_call(head_wgrad_kernel, out_shape=[jax.ShapeDtypeStruct((2 * he...  127 us
    dot_general x3, matrix products, block(): y_b = jnp.einsum('hvt,hvd->td', o_full, w_o, preferred_element_type=F32)  86.4 us
    dot_general x2, matrix products, head_grads(): jnp.einsum('hvd,btd->hbvt', wo_mine, dy, preferred_element_type=F32)  82.8 us
    pallas_call x1, Pallas kernels, down_wgrad(): pl.pallas_call(down_wgrad_kernel, out_shape=[jax.ShapeDtypeStruct((width,...  77.8 us
    all_gather x1, waiting for transfers between devices, block(): draw = lax.all_gather(draw, 'tp', axis=1, tiled=True)  65.9 us
    pallas_call x2, Pallas kernels, fill_other(): pl.pallas_call(fill_kernel, out_shape=jax.ShapeDtypeStruct(whole.shape, w...  48.3 us
  transfers between devices with their start and end apart: 26, of which 11 were waited for; matrix products, arithmetic and copies ran while one was open for 23% of the time, Pallas kernels for 20%

profile of v3, /device:TPU:0, one launch (start us, length us, event | category | flops | bytes accessed | tf_op | source)
XLA Modules:
  0.0 1339.3 jit_solution(9719905160532929623)
XLA Ops:
  7.3 17.1 %fusion.99 = bf16[3,512,576]{2,1,0:T(8,128)(2,1)S(1)} fusion(bf16[3,512,5120]{2,1,0:T(8,128)(2,1)} %param.10, bf16[5120,576]{0,1:T(8,128)(2,1)} %param.14), kind=kOutput, calls=%fused_computation.106 | convolution fusion | flops 9060581376 | bytes 23396352 | tf_op jit(solution)/shard_map/btd,dc->btc/dot_general | solution.py:380
  29.3 32.0 %fusion.16 = (f32[3,512]{1,0:T(4,128)S(1)}, bf16[3,512,1536]{2,1,0:T(8,128)(2,1)S(1)}) fusion(bf16[3,512,5120]{2,1,0:T(8,128)(2,1)} %param.10, bf16[5120,1536]{1,0:T(8,128)(2,1)} %param.12), kind=kOutput, calls=%fused_computation.21 | convolution fusion | flops 24168626176 | bytes 36182016 | tf_op jit(solution)/shard_map/btd,dq->btq/dot_general | solution.py:379
  65.5 41.5 %convert_bitcast_fusion.2.do0_ref = bf16[16,3,128,512]{3,2,1,0:T(8,128)(2,1)} fusion(bf16[3,512,5120]{2,1,0:T(8,128)(2,1)} %in0_ref.1, bf16[32,128,5120]{2,1,0:T(8,128)(2,1)} %param.19, s32[]{:T(128)S(6)} %select_n.59), kind=kOutput, calls=%fused_computation.58 | convolution fusion | flops 32215400448 | bytes 42991620 | tf_op jit(solution)/shard_map/hvd,btd->hbvt/dot_general | solution.py:393
  126.4 11.2 convolution_convert_fusion.v_ref
  137.6 11.3 convolution_convert_fusion.1.k_ref
  148.9 35.0 %convert_bitcast_fusion.q_ref = bf16[16,2,3,192,512]{4,3,2,1,0:T(8,128)(2,1)} fusion(bf16[1,3,512,1536]{3,2,1,0:T(8,128)(2,1)} %bitcast.3, bf16[1,3,512,1536]{3,2,1,0:T(8,128)(2,1)S(1)} %fusion.142, bf16[1536,32,192]{0,2,1:T(8,128)(2,1)} %param.16, s32[]{:T(128)S(6)} %select_n.59), kind=kOutput, calls=%fused_computation.5 | convolution fusion | flops 29019340800 | bytes 37748740 | tf_op jit(solution)/shard_map/heq,sbtq->hsbet/dot_general | solution.py:397
  183.9 41.3 %convert_bitcast_fusion.1.do1_ref = bf16[16,3,128,512]{3,2,1,0:T(8,128)(2,1)} fusion(bf16[3,512,5120]{2,1,0:T(8,128)(2,1)} %collective-permute-done.3.in1_ref, bf16[32,128,5120]{2,1,0:T(8,128)(2,1)} %param.19, s32[]{:T(128)S(6)} %select_n.59), kind=kOutput, calls=%fused_computation.57 | convolution fusion | flops 32215400448 | bytes 42991620 | tf_op jit(solution)/shard_map/hvd,btd->hbvt/dot_general | solution.py:393
  228.0 52.8 %attn_fwd_bwd.3 = (bf16[2,16,128,512]{3,2,1,0:T(8,128)(2,1)S(1)}, bf16[2,16,3,128,512]{4,3,2,1,0:T(8,128)(2,1)}, bf16[2,16,3,192,512]{4,3,2,1,0:T(8,128)(2,1)}, ...) custom-call(s32[1]{0:T(128)} %bitcast.rank_ref, ...), custom_call_target="tpu_custom_call" | custom-call | flops 16777216000 | bytes 33554432 | tf_op jit(solution)/shard_map/attn_fwd_bwd/pallas_call | solution.py:197
  291.4 28.7 %convolution_bitcast_fusion.2 = f32[512,5120]{1,0:T(8,128)} fusion(bf16[32,128,5120]{2,1,0:T(8,128)(2,1)} %param.19, bf16[16,128,512]{2,1,0:T(8,128)(2,1)S(1)} %get-tuple-element.123, bf16[16,128,512]{2,1,0:T(8,128)(2,1)S(1)} %get-tuple-element.122), kind=kOutput, calls=%fused_computation.39 | convolution fusion | flops 21476933632 | bytes 56623104 | tf_op jit(solution)/shard_map/hvt,hvd->td/dot_general | solution.py:413
  323.0 52.5 %attn_fwd_bwd.4 = (bf16[2,16,128,512]{3,2,1,0:T(8,128)(2,1)S(1)}, bf16[2,16,3,128,512]{4,3,2,1,0:T(8,128)(2,1)}, bf16[2,16,3,192,512]{4,3,2,1,0:T(8,128)(2,1)}, ...) custom-call(s32[1]{0:T(128)} %bitcast.rank_ref, ...), custom_call_target="tpu_custom_call", output_to_operand_aliasing={{1}: (9, {}), {2}: (10, {}), {3}: (11, {}), {4}: (12, {})} | custom-call | flops 16777216000 | bytes 33554432 | tf_op jit(solution)/shard_map/attn_fwd_bwd/pallas_call | solution.py:197
  380.2 28.7 %convolution_bitcast_fusion.1 = f32[512,5120]{1,0:T(8,128)} fusion(bf16[32,128,5120]{2,1,0:T(8,128)(2,1)} %param.19, bf16[16,128,512]{2,1,0:T(8,128)(2,1)S(1)} %get-tuple-element.121, bf16[16,128,512]{2,1,0:T(8,128)(2,1)S(1)} %get-tuple-element.120), kind=kOutput, calls=%fused_computation.38 | convolution fusion | flops 21476933632 | bytes 56623104 | tf_op jit(solution)/shard_map/hvt,hvd->td/dot_general | solution.py:413
  411.7 52.4 %attn_fwd_bwd.5 = (bf16[2,16,128,512]{3,2,1,0:T(8,128)(2,1)S(1)}, bf16[2,16,3,128,512]{4,3,2,1,0:T(8,128)(2,1)}, bf16[2,16,3,192,512]{4,3,2,1,0:T(8,128)(2,1)}, ...) custom-call(s32[1]{0:T(128)} %bitcast.rank_ref, ...), custom_call_target="tpu_custom_call", output_to_operand_aliasing={{1}: (9, {}), {2}: (10, {}), {3}: (11, {}), {4}: (12, {})} | custom-call | flops 16777216000 | bytes 33554432 | tf_op jit(solution)/shard_map/attn_fwd_bwd/pallas_call | solution.py:197
  468.7 28.9 %convolution_bitcast_fusion = f32[512,5120]{1,0:T(8,128)} fusion(bf16[32,128,5120]{2,1,0:T(8,128)(2,1)} %param.19, bf16[16,128,512]{2,1,0:T(8,128)(2,1)S(1)} %get-tuple-element.119, bf16[16,128,512]{2,1,0:T(8,128)(2,1)S(1)} %get-tuple-element.118), kind=kOutput, calls=%fused_computation.37 | convolution fusion | flops 21476933632 | bytes 56623104 | tf_op jit(solution)/shard_map/hvt,hvd->td/dot_general | solution.py:413
  497.7 21.7 %fusion.52 = f32[3,512,1536]{2,1,0:T(8,128)} fusion(bf16[1536,32,192]{0,2,1:T(8,128)(2,1)} %param.16, s32[]{:T(128)S(6)} %select_n.59, bf16[2,16,3,192,512]{4,3,2,1,0:T(8,128)(2,1)} %get-tuple-element.97.act_ref), kind=kOutput, calls=%fused_computation.62 | convolution fusion | flops 14495514624 | bytes 28311556 | tf_op jit(solution)/shard_map/hbet,heq->btq/dot_general | solution.py:420
  534.8 8.0 fusion.104
  565.1 21.8 %bitcast_add_fusion = f32[3,512,1536]{2,1,0:T(8,128)S(1)} fusion(f32[3,512,1536]{2,1,0:T(8,128)} %collective-permute-done.7, bf16[1536,32,192]{0,2,1:T(8,128)(2,1)} %param.16, s32[]{:T(128)S(6)} %select_n.59, bf16[2,16,3,192,512]{4,3,2,1,0:T(8,128)(2,1)} %get-tuple-element.97.act_ref), kind=kOutput, calls=%fused_computation.33 | convolution fusion | flops 14497873920 | bytes 37748740 | tf_op jit(solution)/shard_map/hbet,heq->btq/dot_general | solution.py:420
  594.3 84.8 %head_wgrad.3 = (f32[32,128,5120]{2,1,0:T(8,128)}, f32[16,128,5120]{2,1,0:T(8,128)}) custom-call(s32[1]{0:T(128)} %bitcast.rank_ref, bf16[2,16,3,128,512]{4,3,2,1,0:T(8,128)(2,1)} %get-tuple-element.111.act_ref, bf16[3,512,5120]{2,1,0:T(8,128)(2,1)} %in0_ref.1, bf16[3,512,5120]{2,1,0:T(8,128)(2,1)} %collective-permute-done.3.in1_ref), custom_call_target="tpu_custom_call" | custom-call | flops 64424509440 | bytes 83886080 | tf_op jit(solution)/shard_map/head_wgrad/pallas_call | solution.py:280
  682.4 10.5 fusion.87
  695.9 41.7 %head_wgrad.2 = (f32[32,192,1536]{2,1,0:T(8,128)}, f32[16,192,1536]{2,1,0:T(8,128)}) custom-call(s32[1]{0:T(128)} %bitcast.rank_ref, bf16[2,16,3,192,512]{4,3,2,1,0:T(8,128)(2,1)} %get-tuple-element.97.act_ref, bf16[3,512,1536]{2,1,0:T(8,128)(2,1)} %fusion.18.in0_ref, bf16[3,512,1536]{2,1,0:T(8,128)(2,1)} %collective-permute-done.in1_ref), custom_call_target="tpu_custom_call" | custom-call | flops 28991029248 | bytes 37748736 | tf_op jit(solution)/shard_map/head_wgrad/pallas_call | solution.py:280
  738.1 10.6 fusion.92
  760.7 56.2 %reduce-scatter.5.cloned.1.call-done = f32[128,5120]{1,0:T(8,128)} async-done(((f32[512,5120]{1,0:T(8,128)}), f32[128,5120]{1,0:T(8,128)}) %reduce-scatter.5.cloned.1.call-update) | async-done | bytes 2621456 | tf_op jit(solution)/shard_map/reduce_scatter | solution.py:415
  818.8 99.1 %reduce-scatter.7.cloned.1.call-done = f32[128,5120]{1,0:T(8,128)} async-done(((f32[512,5120]{1,0:T(8,128)}), f32[128,5120]{1,0:T(8,128)}) %reduce-scatter.7.cloned.1.call-update) | async-done | bytes 2621456 | tf_op jit(solution)/shard_map/reduce_scatter | solution.py:415
  919.7 99.5 %reduce-scatter.9.cloned.1.call-done = f32[128,5120]{1,0:T(8,128)} async-done(((f32[512,5120]{1,0:T(8,128)}), f32[128,5120]{1,0:T(8,128)}) %reduce-scatter.9.cloned.1.call-update) | async-done | bytes 2621456 | tf_op jit(solution)/shard_map/reduce_scatter | solution.py:415
  1023.3 65.9 %all-gather.3.cloned.1.call-done = bf16[3,512,2112]{2,1,0:T(8,128)(2,1)} async-done(((bf16[3,128,2112]{2,1,0:T(8,128)(2,1)}), bf16[3,512,2112]{2,1,0:T(8,128)(2,1)}) %all-gather.3.cloned.1.call-update) | async-done | bytes 6488080 | tf_op jit(solution)/shard_map/all_gather | solution.py:451
  1097.1 16.5 %fill_other.2 = f32[32,192,1536]{2,1,0:T(8,128)} custom-call(s32[1]{0:T(128)} %bitcast.rank_ref, f32[16,192,1536]{2,1,0:T(8,128)} %collective-permute-done.16.other_ref, f32[32,192,1536]{2,1,0:T(8,128)} %get-tuple-element.108.whole_ref), custom_call_target="tpu_custom_call", output_to_operand_aliasing={{}: (2, {})} | custom-call | flops 3774873600 | bytes 37748736 | tf_op jit(solution)/shard_map/fill_other/pallas_call | solution.py:301
  1113.6 11.6 collective-permute-done.15
  1125.9 7.8 merge_halves.3
  1145.2 34.0 %fusion.8 = f32[3,512,5120]{2,1,0:T(8,128)} fusion(bf16[3,512,1536]{2,1,0:T(8,128)(2,1)} %slice.110, bf16[5120,1536]{1,0:T(8,128)(2,1)} %param.12), kind=kOutput, calls=%fused_computation.10 | convolution fusion | flops 24159191040 | bytes 51904512 | tf_op jit(solution)/shard_map/btq,dq->btd/dot_general | solution.py:470
  1181.4 23.9 %add_convert_fusion = bf16[3,512,5120]{2,1,0:T(8,128)(2,1)} fusion(f32[3,512,5120]{2,1,0:T(8,128)} %fusion.8, bf16[3,512,576]{2,1,0:T(8,128)(2,1)S(1)} %slice.111, bf16[5120,576]{0,1:T(8,128)(2,1)} %param.14), kind=kOutput, calls=%fused_computation | convolution fusion | flops 9075425280 | bytes 54853632 | tf_op jit(solution)/shard_map/btc,dc->btd/dot_general | solution.py:470
  1209.2 77.8 %down_wgrad.1 = (f32[5120,1536]{1,0:T(8,128)}, f32[576,5120]{1,0:T(8,128)}) custom-call(bf16[1536,5120]{1,0:T(8,128)(2,1)} %bitcast.195, bf16[1536,5120]{1,0:T(8,128)(2,1)} %bitcast.58.x1_ref, bf16[1536,1536]{1,0:T(8,128)(2,1)} %bitcast.59.q0_ref, bf16[1536,1536]{1,0:T(8,128)(2,1)} %bitcast.60.q1_ref, bf16[1536,576]{1,0:T(8,128)(2,1)} %bitcast.187, ...), custom_call_target="tpu_custom_call" | custom-call | flops 66437775360 | bytes 74711040 | tf_op jit(solution)/shard_map/down_wgrad/pallas_call | solution.py:330
  1287.0 31.9 %fill_other.3 = f32[32,128,5120]{2,1,0:T(8,128)} custom-call(s32[1]{0:T(128)} %bitcast.rank_ref, f32[16,128,5120]{2,1,0:T(8,128)} %collective-permute-done.19.other_ref, f32[32,128,5120]{2,1,0:T(8,128)} %get-tuple-element.113.whole_ref), custom_call_target="tpu_custom_call", output_to_operand_aliasing={{}: (2, {})} | custom-call | flops 8388608000 | bytes 83886080 | tf_op jit(solution)/shard_map/fill_other/pallas_call | solution.py:301
  1318.9 13.2 copy.112
  (191 shorter events, 154.2 us)
Async XLA Ops:
  7.2 744.5 %reduce-scatter.11.cloned.1.call-start = ((), (), s32[]{:S(2)}) async-start(), calls=%async_computation.7 | async-start | bytes 16711680 | tf_op jit(solution)/shard_map/reduce_scatter | solution.py:432
  24.3 95.9 %copy-start.7 = (bf16[3,512,576]{2,1,0:T(8,128)(2,1)}, bf16[3,512,576]{2,1,0:T(8,128)(2,1)S(1)}, u32[]{:S(2)}) copy-start(bf16[3,512,576]{2,1,0:T(8,128)(2,1)S(1)} %fusion.99) | copy-start | bytes 5308420
  26.4 99.6 %collective-permute-start.2 = (bf16[3,512,64]{2,1,0:T(8,128)(2,1)S(1)}, bf16[3,512,64]{2,1,0:T(8,128)(2,1)S(1)}, u32[]{:S(2)}, u32[]{:S(2)}) collective-permute-start(bf16[3,512,64]{2,1,0:T(8,128)(2,1)S(1)} %pad_maximum_fusion.5), channel_id=1, source_target_pairs={{0,1},{1,0},{2,3},{3,2},{4,5},{5,4},{6,7},{7,6}} | collective-permute-start | bytes 589832 | tf_op jit(solution)/shard_map/ppermute | solution.py:349
  29.3 32.0 %copy-start.29 = (bf16[1536]{0:T(1024)(128)(2,1)S(1)}, bf16[1536]{0:T(1024)(128)(2,1)}, u32[]{:S(2)}) copy-start(bf16[1536]{0:T(1024)(128)(2,1)} %param.13) | copy-start | bytes 9220
  29.3 97.1 %collective-permute-start.1 = (bf16[3,512,512]{2,1,0:T(8,128)(2,1)}, bf16[3,512,512]{2,1,0:T(8,128)(2,1)}, u32[]{:S(2)}, u32[]{:S(2)}) collective-permute-start(bf16[3,512,512]{2,1,0:T(8,128)(2,1)} %fusion.79), channel_id=1, source_target_pairs={{0,1},{1,0},{2,3},{3,2},{4,5},{5,4},{6,7},{7,6}} | collective-permute-start | bytes 4718600 | tf_op jit(solution)/shard_map/ppermute | solution.py:349
  61.3 60.1 %copy-start.23 = (f32[1536]{0:T(1024)}, f32[1536]{0:T(1024)S(1)}, u32[]{:S(2)}) copy-start(f32[1536]{0:T(1024)S(1)} %convert_element_type.102) | copy-start | bytes 18436
  65.0 83.9 %collective-permute-start = (bf16[3,512,1536]{2,1,0:T(8,128)(2,1)}, bf16[3,512,1536]{2,1,0:T(8,128)(2,1)}, u32[]{:S(2)}, u32[]{:S(2)}) collective-permute-start(bf16[3,512,1536]{2,1,0:T(8,128)(2,1)} %fusion.18.in0_ref), channel_id=1, source_target_pairs={{0,1},{1,0},{2,3},{3,2},{4,5},{5,4},{6,7},{7,6}} | collective-permute-start | bytes 14155784 | tf_op jit(solution)/shard_map/ppermute | solution.py:349
  65.5 118.4 %collective-permute-start.3 = (bf16[3,512,5120]{2,1,0:T(8,128)(2,1)}, bf16[3,512,5120]{2,1,0:T(8,128)(2,1)}, u32[]{:S(2)}, u32[]{:S(2)}) collective-permute-start(bf16[3,512,5120]{2,1,0:T(8,128)(2,1)} %in0_ref.1), channel_id=1, source_target_pairs={{0,1},{1,0},{2,3},{3,2},{4,5},{5,4},{6,7},{7,6}} | collective-permute-start | bytes 47185928 | tf_op jit(solution)/shard_map/ppermute | solution.py:349
  284.3 4.6 collective-permute-start.4
  375.7 4.2 collective-permute-start.5
  464.3 4.2 collective-permute-start.6
  519.3 45.8 %collective-permute-start.7 = (f32[3,512,1536]{2,1,0:T(8,128)}, f32[3,512,1536]{2,1,0:T(8,128)}, u32[]{:S(2)}, u32[]{:S(2)}) collective-permute-start(f32[3,512,1536]{2,1,0:T(8,128)} %fusion.52), channel_id=1, source_target_pairs={{0,1},{1,0},{2,3},{3,2},{4,5},{5,4},{6,7},{7,6}} | collective-permute-start | bytes 28311560 | tf_op jit(solution)/shard_map/ppermute | solution.py:349
  542.8 14.8 %collective-permute-start.8 = (f32[3,512,512]{2,1,0:T(8,128)}, f32[3,512,512]{2,1,0:T(8,128)}, u32[]{:S(2)}, u32[]{:S(2)}) collective-permute-start(f32[3,512,512]{2,1,0:T(8,128)} %fusion.104), channel_id=1, source_target_pairs={{0,1},{1,0},{2,3},{3,2},{4,5},{5,4},{6,7},{7,6}} | collective-permute-start | bytes 9437192 | tf_op jit(solution)/shard_map/ppermute | solution.py:349
  544.5 4.9 collective-permute-start.9
  592.2 224.7 %reduce-scatter.5.cloned.1.call-start = ((), (), s32[]{:S(2)}) async-start(), calls=%async_computation.4 | async-start | bytes 13107200 | tf_op jit(solution)/shard_map/reduce_scatter | solution.py:415
  592.9 324.9 %reduce-scatter.7.cloned.1.call-start = ((), (), s32[]{:S(2)}) async-start(), calls=%async_computation.5 | async-start | bytes 13107200 | tf_op jit(solution)/shard_map/reduce_scatter | solution.py:415
  593.7 425.6 %reduce-scatter.9.cloned.1.call-start = ((), (), s32[]{:S(2)}) async-start(), calls=%async_computation.6 | async-start | bytes 13107200 | tf_op jit(solution)/shard_map/reduce_scatter | solution.py:415
  594.2 84.9 %copy-start.8 = (bf16[3,512,576]{2,1,0:T(8,128)(2,1)S(1)}, bf16[3,512,576]{2,1,0:T(8,128)(2,1)}, u32[]{:S(2)}) copy-start(bf16[3,512,576]{2,1,0:T(8,128)(2,1)} %copy-done.7) | copy-start | bytes 5308420
  594.2 88.2 %copy-start.18 = (bf16[1,3,512,512]{3,2,1,0:T(8,128)(2,1)S(1)}, bf16[1,3,512,512]{3,2,1,0:T(8,128)(2,1)}, u32[]{:S(2)}) copy-start(bf16[1,3,512,512]{3,2,1,0:T(8,128)(2,1)} %copy-done.17) | copy-start | bytes 4718596
  594.2 494.9 %all-gather.3.cloned.1.call-start = ((), (), s32[]{:S(2)}) async-start(), calls=%async_computation.8 | async-start | bytes 8355840 | tf_op jit(solution)/shard_map/all_gather | solution.py:451
  679.1 607.9 %collective-permute-start.19 = (f32[16,128,5120]{2,1,0:T(8,128)}, f32[16,128,5120]{2,1,0:T(8,128)}, u32[]{:S(2)}, u32[]{:S(2)}) collective-permute-start(f32[16,128,5120]{2,1,0:T(8,128)} %get-tuple-element.112), channel_id=1, source_target_pairs={{0,1},{1,0},{2,3},{3,2},{4,5},{5,4},{6,7},{7,6}} | collective-permute-start | bytes 125829128 | tf_op jit(solution)/shard_map/ppermute | solution.py:349
  737.6 359.0 %collective-permute-start.16 = (f32[16,192,1536]{2,1,0:T(8,128)}, f32[16,192,1536]{2,1,0:T(8,128)}, u32[]{:S(2)}, u32[]{:S(2)}) collective-permute-start(f32[16,192,1536]{2,1,0:T(8,128)} %get-tuple-element.107), channel_id=1, source_target_pairs={{0,1},{1,0},{2,3},{3,2},{4,5},{5,4},{6,7},{7,6}} | collective-permute-start | bytes 56623112 | tf_op jit(solution)/shard_map/ppermute | solution.py:349
  760.7 558.2 %all-gather.5.cloned.1.call-start = ((), (), s32[]{:S(2)}) async-start(), calls=%async_computation.9 | async-start | bytes 19660800 | tf_op jit(solution)/shard_map/all_gather | solution.py:459
  1089.2 120.0 %collective-permute-start.10 = (bf16[3,512,5120]{2,1,0:T(8,128)(2,1)}, bf16[3,512,5120]{2,1,0:T(8,128)(2,1)}, u32[]{:S(2)}, u32[]{:S(2)}) collective-permute-start(bf16[3,512,5120]{2,1,0:T(8,128)(2,1)} %param.10), channel_id=1, source_target_pairs={{0,1},{1,0},{2,3},{3,2},{4,5},{5,4},{6,7},{7,6}} | collective-permute-start | bytes 47185928 | tf_op jit(solution)/shard_map/ppermute | solution.py:349
  1089.3 3.7 collective-permute-start.13
  1090.8 35.1 %collective-permute-start.18 = (f32[512,16,128]{2,1,0:T(8,128)}, f32[512,16,128]{2,1,0:T(8,128)}, u32[]{:S(2)}, u32[]{:S(2)}) collective-permute-start(f32[512,16,128]{2,1,0:T(8,128)} %bitcast.181), channel_id=1, source_target_pairs={{0,1},{1,0},{2,3},{3,2},{4,5},{5,4},{6,7},{7,6}} | collective-permute-start | bytes 12582920 | tf_op jit(solution)/shard_map/ppermute | solution.py:349
  1093.0 3.7 collective-permute-start.14
  1096.6 37.1 %collective-permute-start.17 = (f32[512,16,128]{2,1,0:T(8,128)}, f32[512,16,128]{2,1,0:T(8,128)}, u32[]{:S(2)}, u32[]{:S(2)}) collective-permute-start(f32[512,16,128]{2,1,0:T(8,128)} %bitcast.179), channel_id=1, source_target_pairs={{0,1},{1,0},{2,3},{3,2},{4,5},{5,4},{6,7},{7,6}} | collective-permute-start | bytes 12582920 | tf_op jit(solution)/shard_map/ppermute | solution.py:349
  1096.6 28.6 %collective-permute-start.15 = (f32[2048]{0:T(1024)S(1)}, f32[2048]{0:T(1024)S(1)}, u32[]{:S(2)}, u32[]{:S(2)}) collective-permute-start(f32[2048]{0:T(1024)S(1)} %add.123), channel_id=1, source_target_pairs={{0,1},{1,0},{2,3},{3,2},{4,5},{5,4},{6,7},{7,6}} | collective-permute-start | bytes 24584 | tf_op jit(solution)/shard_map/ppermute | solution.py:349
  1145.1 36.2 %copy-start.10 = (bf16[3,512,576]{2,1,0:T(8,128)(2,1)}, bf16[3,512,576]{2,1,0:T(8,128)(2,1)S(1)}, u32[]{:S(2)}) copy-start(bf16[3,512,576]{2,1,0:T(8,128)(2,1)S(1)} %slice.111) | copy-start | bytes 5308420
  1145.1 64.1 %collective-permute-start.11 = (bf16[3,512,1536]{2,1,0:T(8,128)(2,1)}, bf16[3,512,1536]{2,1,0:T(8,128)(2,1)}, u32[]{:S(2)}, u32[]{:S(2)}) collective-permute-start(bf16[3,512,1536]{2,1,0:T(8,128)(2,1)} %slice.110), channel_id=1, source_target_pairs={{0,1},{1,0},{2,3},{3,2},{4,5},{5,4},{6,7},{7,6}} | collective-permute-start | bytes 14155784 | tf_op jit(solution)/shard_map/ppermute | solution.py:349
  1181.4 23.9 %collective-permute-start.12 = (bf16[3,512,576]{1,2,0:T(8,128)(2,1)}, bf16[3,512,576]{1,2,0:T(8,128)(2,1)}, u32[]{:S(2)}, u32[]{:S(2)}) collective-permute-start(bf16[3,512,576]{1,2,0:T(8,128)(2,1)} %copy.60), channel_id=1, source_target_pairs={{0,1},{1,0},{2,3},{3,2},{4,5},{5,4},{6,7},{7,6}} | collective-permute-start | bytes 5308424 | tf_op jit(solution)/shard_map/ppermute | solution.py:349
  (29 other events, 180.8 us)
Sparse Core Ops, SparseCore 0:
  592.3 123.5 reduce-scatter.10
  718.9 97.8 reduce-scatter.4
  819.9 97.8 reduce-scatter.6
  921.3 97.8 reduce-scatter.8
  1021.4 67.7 all-gather.2
  1090.8 142.9 all-gather.4
